TPU v7x, 32 devices: a whole 2x2x4 slice. The times are simulated.
32 devices in a mesh: dp: 4 (over x, core), seq: 4 (over z), tensor: 2 (over y).
Axes of the slice: x: 2, y: 2, z: 4, core: 2. Of those that a mesh axis runs over, the one named last changes fastest.
Arguments:
- query_vectors: bfloat16 [896, 4096], P(('dp', 'seq'), 'tensor'), may hold values from -128 to 128
- key_vectors: bfloat16 [896, 2048], P(('dp', 'seq'), 'tensor'), may hold values from -6 to 6
- value_vectors: bfloat16 [896, 2048], P(('dp', 'seq'), 'tensor'), may hold values from -6 to 6
- out_weight: bfloat16 [4096, 3584], P(None, 'tensor'), may hold values from -0.09375 to 0.09375
- residual: bfloat16 [896, 3584], P(('dp', 'seq'), 'tensor'), may hold values from -64 to 64
- post_gain: float32 [3584], P('tensor'), may hold values from 0.1 to 1.9
- final_gain: float32 [3584], P('tensor'), may hold values from 0.1 to 1.9
- vocab_weight: bfloat16 [16000, 3584], P(('dp', 'seq', 'tensor')), may hold values from -4 to 4
- segment_ids: int32 [4, 224], P('dp', 'seq'), may hold values from 0 to 7, as said below
- doc_starts: int32 [4, 8], P('dp'), may hold values from 0 to 223, as said below
- doc_index: int32 [4, 8], P('dp'), may hold values from 0 to 31
- targets: int32 [4, 224], replicated, may hold values from 0 to 15999
Outputs:
- token_logprob: float32 [4, 224], P('dp', 'seq')
- doc_loglik: float32 [32], replicated
- doc_counts: float32 [32], replicated
Inputs may be any that keep to these rules, and one draw needn't show every extreme that they name: `segment_ids`: within each row the numbers never fall and every number 0 to 7 appears; segment s of a row begins at doc_starts[row, s]; each segment holds 1 to 168 positions. doc_starts[row, 0] = 0 and the starts rise strictly along each row.
All inputs are finite; a program needn't handle non-finite values.
Results may differ from a plain program's by a relative error of at most 0.00074.
Values may be sent and summed in bfloat16 or wider, within the bound.
A program may use at most 64 MiB of HBM per device.

v0:
```python
import functools

import jax
import jax.numpy as jnp
from jax import lax
from jax.experimental import pallas as pl
from jax.experimental.pallas import tpu as pltpu
from jax.sharding import PartitionSpec as P

HEAD_DIM = 256
ATTENTION_CAP = 50.0
LOGIT_CAP = 30.0
EPSILON = 1e-06
MESH = pl.DeviceIdType.MESH
PAD = 64
NT = (((1,), (1,)), ((), ()))
NN = (((1,), (0,)), ((), ()))


def dot(a, b, dims):
    return lax.dot_general(a, b, dims, preferred_element_type=jnp.float32)


def body(
    sizes,
    q_ref, k_ref, v_ref, w_hbm, res_ref, pg_ref, fg_ref, voc_hbm, seg_ref, start_ref, index_ref, target_ref,
    lp_ref, like_ref, cnt_ref,
    w_ref, voc_ref, kv, num, den, att, branch, stat, hid, held, lab_ref, part, gat_dp, gat_t, gat_s,
    local_sem, kv_send, kv_recv, att_send, att_recv, st_send, st_recv,
    hid_recv, z_send, y_send, x_send, c_send,
    fd_send, fd_recv, ft_send, ft_recv, fs_send, fs_recv,
):
    ND, NZ, NY, docs = sizes
    NC = 2 if ND % 2 == 0 else 1
    NX = ND // NC
    D = voc_hbm.shape[-1] if voc_hbm.ndim == 2 else voc_hbm.shape[0] * voc_hbm.shape[2]
    me_d, me_z, me_t = lax.axis_index("dp"), lax.axis_index("seq"), lax.axis_index("tensor")
    me_x, me_c = me_d // NC, me_d % NC
    rows = q_ref.shape[0]
    kvw = k_ref.shape[1]
    groups = kvw // HEAD_DIM
    per = q_ref.shape[1] // kvw
    heads = groups * per
    qw = q_ref.shape[1]
    fw = w_hbm.shape[1]

    w_copy = pltpu.make_async_copy(w_hbm, w_ref, local_sem.at[0])
    voc_copy = pltpu.make_async_copy(voc_hbm, voc_ref, local_sem.at[1])
    w_copy.start()
    voc_copy.start()

    def dev(d=None, z=None, t=None):
        return (me_d if d is None else d, me_z if z is None else z, me_t if t is None else t)

    def remote(src, dst, send, recv, device):
        return pltpu.make_async_remote_copy(
            src_ref=src, dst_ref=dst, send_sem=send, recv_sem=recv, device_id=device, device_id_type=MESH
        )

    def others(me, n):
        return [lax.rem(me + i, n) for i in range(1, n)]

    barrier = pltpu.get_barrier_semaphore()
    peers = [dev(d=p) for p in others(me_d, ND)]
    peers += [dev(z=p) for p in others(me_z, NZ)]
    peers += [dev(t=p) for p in others(me_t, NY)]
    for p in peers:
        pl.semaphore_signal(barrier, inc=1, device_id=p, device_id_type=MESH)
    pl.semaphore_wait(barrier, len(peers))

    def kv_copy(block, g):
        cols = pl.ds(g * HEAD_DIM, HEAD_DIM)
        up = dev(z=lax.rem(me_z + 1, NZ))
        if block is None:
            pairs = [(k_ref.at[:, cols], kv.at[me_z, 0, :, cols]), (v_ref.at[:, cols], kv.at[me_z, 1, :, cols])]
            where = me_z
        else:
            pairs = [(kv.at[block, i, :, cols],) * 2 for i in range(2)]
            where = block
        return [
            remote(src, dst, kv_send.at[where, g, i], kv_recv.at[where, g, i], up)
            for i, (src, dst) in enumerate(pairs)
        ]

    @pl.when(me_z + 1 < NZ)
    def _():
        for g in range(groups):
            for c in kv_copy(None, g):
                c.start()

    seg = seg_ref[...]
    first_row = jnp.zeros((1, rows), jnp.int32)
    end_row = jnp.zeros((1, rows), jnp.int32)
    doc_row = jnp.zeros((1, rows), jnp.int32)
    segs = start_ref.shape[1]
    for n in range(segs):
        here = seg == n
        first_row = jnp.where(here, start_ref[0, n], first_row)
        end_row = jnp.where(here, start_ref[0, n + 1] if n + 1 < segs else rows * NZ, end_row)
        doc_row = jnp.where(here, index_ref[0, n], doc_row)
    spot = me_z * rows + lax.broadcasted_iota(jnp.int32, (1, rows), 1)
    code_row = doc_row + jnp.where(spot + 1 < end_row, docs, 0)
    i_pos = lax.broadcasted_iota(jnp.int32, (rows, rows), 0)
    j_pos = lax.broadcasted_iota(jnp.int32, (rows, rows), 1)

    def column_of(row):
        full = jnp.broadcast_to(row.astype(jnp.float32), (rows, rows))
        return jnp.sum(jnp.where(i_pos == j_pos, full, 0.0), axis=1, keepdims=True)

    first = column_of(first_row).astype(jnp.int32)
    per_line = 128 // PAD
    my_block = me_d * NZ + me_z
    lanes = lax.broadcasted_iota(jnp.int32, (rows, 128), 1)
    sub = lax.broadcasted_iota(jnp.int32, (rows, 128), 0)
    placed = jnp.where(lanes == sub + lax.rem(my_block, per_line) * PAD, column_of(code_row), 0.0)
    code_line = jnp.sum(placed, axis=0, keepdims=True) * jnp.where(me_t == 0, 1.0, 0.0)
    gap = jnp.zeros((1, PAD - rows), jnp.int32)
    for d in range(ND):
        pieces = []
        for z in range(NZ):
            pieces += [target_ref[d:d + 1, z * rows:(z + 1) * rows], gap]
        lab_ref[d] = jnp.concatenate(pieces, axis=1)

    def attend(block, g):
        cols = slice(g * HEAD_DIM, (g + 1) * HEAD_DIM)
        if block is None:
            kk, vv = k_ref[:, cols], v_ref[:, cols]
            seen = (me_z * rows + j_pos >= first) & (j_pos <= i_pos)
        else:
            kk, vv = kv[block, 0, :, cols], kv[block, 1, :, cols]
            seen = block * rows + j_pos >= first
        for h in range(g * per, (g + 1) * per):
            raw = dot(q_ref[:, h * HEAD_DIM:(h + 1) * HEAD_DIM], kk, NT)
            capped = ATTENTION_CAP * jnp.tanh(raw * (HEAD_DIM ** (-0.5) / ATTENTION_CAP))
            wt = jnp.where(seen, jnp.exp(capped), 0.0)
            top = dot(wt.astype(jnp.bfloat16), vv, NN)
            low = jnp.broadcast_to(jnp.sum(wt, axis=1, keepdims=True), (rows, 128))
            if block is None:
                num[h] = top
                den[h] = low
            else:
                num[h] = num[h] + top
                den[h] = den[h] + low

    def arrived(block, g):
        for c in kv_copy(block, g):
            c.wait_recv()

        @pl.when(me_z + 1 < NZ)
        def _():
            for c in kv_copy(block, g):
                c.start()

    for g in range(groups):
        attend(None, g)
    for block in range(NZ - 2, 0, -1):
        @pl.when(block < me_z)
        def _(block=block):
            for g in range(groups):
                arrived(block, g)
                attend(block, g)

    gw = per * HEAD_DIM

    def att_copy(g, peer, idx):
        ref = att.at[me_t, :, pl.ds(g * gw, gw)]
        return remote(ref, ref, att_send.at[idx, g], att_recv.at[me_t, g], dev(t=peer))

    step = 256 if fw % 256 == 0 else fw

    def project(t, g, begin):
        base = pl.multiple_of(t * qw + g * gw, gw)
        left = att[t, :, g * gw:(g + 1) * gw]
        for n in range(fw // step):
            cols = slice(n * step, (n + 1) * step)
            got = dot(left, w_ref[pl.ds(base, gw), cols], NN)
            branch[:, cols] = got if begin else branch[:, cols] + got

    for g in range(groups):
        if NZ > 1:
            @pl.when(me_z > 0)
            def _(g=g):
                arrived(0, g)
                attend(0, g)
        for h in range(g * per, (g + 1) * per):
            att[me_t, :, h * HEAD_DIM:(h + 1) * HEAD_DIM] = (num[h] / den[h][:, :1]).astype(jnp.bfloat16)
        for i, p in enumerate(others(me_t, NY)):
            att_copy(g, p, i).start()
        if g == 0:
            w_copy.wait()
        project(me_t, g, g == 0)
    for g in range(groups):
        for p in others(me_t, NY):
            ref = att.at[p, :, pl.ds(g * gw, gw)]
            remote(ref, ref, att_send.at[0, 0], att_recv.at[p, g], dev()).wait_recv()
            project(p, g, False)

    br = branch[...]
    carried = res_ref[...].astype(jnp.float32)
    gained = pg_ref[...].reshape(1, fw) * br
    lane = lax.broadcasted_iota(jnp.int32, (rows, 128), 1)
    packed = jnp.zeros((rows, 128), jnp.float32)
    for i, prod in enumerate((br * br, carried * carried, carried * gained, gained * gained)):
        packed = jnp.where(lane == i, jnp.sum(prod, axis=1, keepdims=True), packed)
    stat[me_t] = packed

    def stat_copy(peer, i):
        return remote(stat.at[me_t], stat.at[me_t], st_send.at[i], st_recv.at[me_t], dev(t=peer))

    for i, p in enumerate(others(me_t, NY)):
        stat_copy(p, i).start()
    for p in others(me_t, NY):
        remote(stat.at[p], stat.at[p], st_send.at[0], st_recv.at[p], dev()).wait_recv()
    total = stat[0]
    for t in range(1, NY):
        total = total + stat[t]
    sq_branch, sq_carried, cross, sq_gained = (total[:, i:i + 1] for i in range(4))
    inv_branch = 1.0 / jnp.sqrt(sq_branch / D + EPSILON)
    sq_total = sq_carried + 2.0 * inv_branch * cross + inv_branch * inv_branch * sq_gained
    inv_total = 1.0 / jnp.sqrt(sq_total / D + EPSILON)
    hid[me_d, me_z, me_t, :rows, :] = (
        fg_ref[...].reshape(1, fw) * (carried + gained * inv_branch) * inv_total
    ).astype(jnp.bfloat16)

    def slot(d, z, t):
        return hid.at[d, z, t, pl.ds(0, rows), :]

    def send(d, z, t, sem, device):
        return remote(slot(d, z, t), slot(d, z, t), sem, hid_recv.at[d, z, t], device)

    def landed(d, z, t):
        send(d, z, t, z_send.at[0, 0], dev()).wait_recv()

    y_peers = others(me_t, NY)
    x_peers = [p * NC + me_c for p in others(me_x, NX)]
    twin = [me_x * NC + 1 - me_c] if NC == 2 else []
    offsets = [0]
    for i in range(1, NZ):
        offsets += [-i, i]

    def y_first(z):
        return lax.rem(z + me_c, 2) == 0

    def guarded(off, fn):
        if off == 0:
            fn(me_z)
        else:
            @pl.when((me_z + off >= 0) & (me_z + off < NZ))
            def _():
                fn(me_z + off)

    def to_twin(d, z, t, act):
        for p in twin:
            act(send(d, z, t, c_send.at[d // NC, z, t], dev(d=p)))

    def column(z, off, act, wait):
        if wait and off != 0:
            landed(me_d, z, me_t)
        if off <= 0:
            @pl.when(me_z + 1 < NZ)
            def _():
                act(send(me_d, z, me_t, z_send.at[z, 0], dev(z=lax.rem(me_z + 1, NZ))))
        if off >= 0:
            @pl.when(me_z >= 1)
            def _():
                act(send(me_d, z, me_t, z_send.at[z, 1], dev(z=lax.rem(me_z + NZ - 1, NZ))))
        for i, p in enumerate(y_peers):
            act(send(me_d, z, me_t, y_send.at[0, z, i], dev(t=p)))
        for i, p in enumerate(x_peers):
            act(send(me_d, z, me_t, x_send.at[0, z, i], dev(d=p)))
        to_twin(me_d, z, me_t, act)

    def across(z, act, wait):
        for j, t in enumerate(y_peers):
            if wait:
                landed(me_d, z, t)
            if x_peers:
                @pl.when(y_first(z))
                def _(j=j, t=t):
                    for i, p in enumerate(x_peers):
                        act(send(me_d, z, t, x_send.at[1 + j, z, i], dev(d=p)))
            to_twin(me_d, z, t, act)
        for j, d in enumerate(x_peers):
            if wait:
                landed(d, z, me_t)
            if y_peers:
                @pl.when(jnp.logical_not(y_first(z)))
                def _(j=j, d=d):
                    for i, p in enumerate(y_peers):
                        act(send(d, z, me_t, y_send.at[1 + j, z, i], dev(t=p)))
            to_twin(d, z, me_t, act)

    def diagonal(z, act, wait):
        for d in x_peers:
            for t in y_peers:
                if wait:
                    landed(d, z, t)
                to_twin(d, z, t, act)

    def start(c):
        c.start()

    guarded(offsets[0], lambda z: column(z, 0, start, True))
    for n in range(1, len(offsets) + 1):
        if n < len(offsets):
            guarded(offsets[n], lambda z: column(z, offsets[n], start, True))
        guarded(offsets[n - 1], lambda z: across(z, start, True))

    voc_copy.wait()
    count = voc_ref.shape[-2]
    base = ((me_d * NZ + me_z) * NY + me_t) * count
    vocab_ids = base + lax.broadcasted_iota(jnp.int32, (count, NZ * PAD), 0)
    per_row = NZ * PAD // 128
    R = ND * per_row

    def product(d, t):
        if len(voc_ref.shape) == 2:
            start_col = t * fw if isinstance(t, int) else pl.multiple_of(t * fw, 128)
            left = voc_ref[:, pl.ds(start_col, fw)]
        else:
            left = voc_ref[t]
        return dot(left, hid[d, :, t].reshape(NZ * PAD, fw), NT)

    def finish(d, acc):
        capped = LOGIT_CAP * jnp.tanh(acc * (1.0 / LOGIT_CAP))
        tot = jnp.sum(jnp.exp(capped), axis=0, keepdims=True)
        cho = jnp.sum(jnp.where(vocab_ids == lab_ref[d], capped, 0.0), axis=0, keepdims=True)
        for r in range(per_row):
            part[pl.ds(d * per_row + r, 1), :] = tot[:, r * 128:(r + 1) * 128]
            part[pl.ds(R + d * per_row + r, 1), :] = cho[:, r * 128:(r + 1) * 128]

    def logits_of(d):
        acc = product(d, 0)
        for t in range(1, NY):
            acc = acc + product(d, t)
        finish(d, acc)

    part[2 * R:3 * R, :] = jnp.zeros((R, 128), jnp.float32)
    part[pl.ds(2 * R + my_block // per_line, 1), :] = code_line
    logits_of(me_d)
    for d in twin:
        for z in range(NZ):
            for t in range(NY):
                landed(d, z, t)
        logits_of(d)
    far = [p * NC + 1 - me_c for p in others(me_x, NX)] if NC == 2 else []
    for i, d in enumerate(x_peers):
        held[i] = product(d, me_t)
    for i, d in enumerate(far):
        for z in range(NZ):
            landed(d, z, me_t)
        held[NX - 1 + i] = product(d, me_t)
    for off in offsets:
        guarded(off, lambda z: diagonal(z, start, True))
    for i, d in enumerate(x_peers):
        acc = held[i]
        for t in y_peers:
            acc = acc + product(d, t)
        finish(d, acc)
    for i, d in enumerate(far):
        acc = held[NX - 1 + i]
        for t in y_peers:
            for z in range(NZ):
                landed(d, z, t)
            acc = acc + product(d, t)
        finish(d, acc)

    def exchange(buf, me, n, sends, recvs, where):
        buf[me] = part[...]

        def copy(p, i):
            return remote(buf.at[me], buf.at[me], sends.at[i], recvs.at[me], where(p))

        for i, p in enumerate(others(me, n)):
            copy(p, i).start()
        for p in others(me, n):
            remote(buf.at[p], buf.at[p], sends.at[0], recvs.at[p], dev()).wait_recv()
        out = buf[0]
        for j in range(1, n):
            out = out + buf[j]
        part[...] = out
        return lambda: [copy(p, i).wait_send() for i, p in enumerate(others(me, n))]

    drains = [
        exchange(gat_dp, me_d, ND, fd_send, fd_recv, lambda p: dev(d=p)),
        exchange(gat_t, me_t, NY, ft_send, ft_recv, lambda p: dev(t=p)),
        exchange(gat_s, me_z, NZ, fs_send, fs_recv, lambda p: dev(z=p)),
    ]
    totals, chosen = part[0:R, :], part[R:2 * R, :]
    code = part[2 * R:3 * R, :]
    inside = lax.rem(lax.broadcasted_iota(jnp.int32, (R, 128), 1), PAD) < rows
    counted = jnp.where(inside & (code >= docs), 1.0, 0.0)
    doc = jnp.where(code >= docs, code - docs, code)
    logprob = jnp.where(inside, counted * (chosen - jnp.log(totals)), 0.0)
    part[0:R, :] = logprob
    line = part[pl.ds(my_block // per_line, 1), :]
    mine = line[:, :rows]
    for k in range(1, per_line):
        mine = jnp.where(lax.rem(my_block, per_line) == k, line[:, k * PAD:k * PAD + rows], mine)
    lp_ref[...] = mine
    names = lax.broadcasted_iota(jnp.int32, (docs, 128), 0).astype(jnp.float32)
    like = jnp.zeros((docs, 128), jnp.float32)
    cnt = jnp.zeros((docs, 128), jnp.float32)
    for r in range(R):
        hit = names == doc[r:r + 1, :]
        like = like + jnp.where(hit, logprob[r:r + 1, :], 0.0)
        cnt = cnt + jnp.where(hit, counted[r:r + 1, :], 0.0)
    eye = lax.broadcasted_iota(jnp.int32, (docs, docs), 0) == lax.broadcasted_iota(jnp.int32, (docs, docs), 1)
    for out, sums in ((like_ref, like), (cnt_ref, cnt)):
        tall = jnp.sum(sums, axis=1, keepdims=True)
        out[...] = jnp.sum(jnp.where(eye, tall, 0.0), axis=0, keepdims=True)

    def drain(c):
        c.wait_send()

    for block in [None, *range(NZ - 1)]:
        @pl.when((me_z + 1 < NZ) if block is None else (me_z > block) & (me_z + 1 < NZ))
        def _(block=block):
            for g in range(groups):
                for c in kv_copy(block, g):
                    c.wait_send()
    for i, p in enumerate(others(me_t, NY)):
        for g in range(groups):
            att_copy(g, p, i).wait_send()
        stat_copy(p, i).wait_send()
    for off in offsets:
        guarded(off, lambda z: column(z, off, drain, False))
        guarded(off, lambda z: across(z, drain, False))
        guarded(off, lambda z: diagonal(z, drain, False))
    for d in drains:
        d()


def local(
    mesh, query_vectors, key_vectors, value_vectors, out_weight, residual, post_gain, final_gain,
    vocab_weight, segment_ids, doc_starts, doc_index, targets,
):
    ND, NZ, NY = mesh.shape["dp"], mesh.shape["seq"], mesh.shape["tensor"]
    rows = query_vectors.shape[0]
    docs = doc_starts.shape[1] * ND
    blocks = ND * NZ
    fw = out_weight.shape[1]
    voc = vocab_weight
    if fw % 128 != 0:
        voc = voc.reshape(voc.shape[0], NY, fw).transpose(1, 0, 2)
    kvw, qw = key_vectors.shape[1], query_vectors.shape[1]
    heads = qw // HEAD_DIM
    groups = kvw // HEAD_DIM
    NC = 2 if ND % 2 == 0 else 1
    NX = ND // NC
    R = blocks * PAD // 128
    f32, bf16 = jnp.float32, jnp.bfloat16
    dma = pltpu.SemaphoreType.DMA
    vm = pl.BlockSpec(memory_space=pltpu.VMEM)
    anyspace = pl.BlockSpec(memory_space=pl.ANY)
    smem = pl.BlockSpec(memory_space=pltpu.SMEM)
    sums = jax.ShapeDtypeStruct((1, docs), f32)
    logprob, like, counts = pl.pallas_call(
        functools.partial(body, (ND, NZ, NY, docs)),
        out_shape=(jax.ShapeDtypeStruct((1, rows), f32), sums, sums),
        in_specs=[vm, vm, vm, anyspace, vm, vm, vm, anyspace, vm, smem, smem, vm],
        out_specs=(vm, vm, vm),
        scratch_shapes=[
            pltpu.VMEM(out_weight.shape, bf16),
            pltpu.VMEM(voc.shape, bf16),
            pltpu.VMEM((NZ, 2, rows, kvw), bf16),
            pltpu.VMEM((heads, rows, HEAD_DIM), f32),
            pltpu.VMEM((heads, rows, 128), f32),
            pltpu.VMEM((NY, rows, qw), bf16),
            pltpu.VMEM((rows, fw), f32),
            pltpu.VMEM((NY, rows, 128), f32),
            pltpu.VMEM((ND, NZ, NY, PAD, fw), bf16),
            pltpu.VMEM((ND - NC, voc.shape[-2], NZ * PAD), f32),
            pltpu.VMEM((ND, 1, NZ * PAD), jnp.int32),
            pltpu.VMEM((3 * R, 128), f32),
            pltpu.VMEM((ND, 3 * R, 128), f32),
            pltpu.VMEM((NY, 3 * R, 128), f32),
            pltpu.VMEM((NZ, 3 * R, 128), f32),
            dma((2,)),
            dma((NZ, groups, 2)), dma((NZ, groups, 2)),
            dma((NY, groups)), dma((NY, groups)),
            dma((NY,)), dma((NY,)),
            dma((ND, NZ, NY)),
            dma((NZ, 2)),
            dma((NX, NZ, NY)),
            dma((NY, NZ, NX)),
            dma((NX, NZ, NY)),
            dma((ND,)), dma((ND,)),
            dma((NY,)), dma((NY,)),
            dma((NZ,)), dma((NZ,)),
        ],
        compiler_params=pltpu.CompilerParams(
            collective_id=0, has_side_effects=True, vmem_limit_bytes=60 * 1024 * 1024
        ),
        name="packed_loglik",
    )(
        query_vectors, key_vectors, value_vectors, out_weight, residual, post_gain, final_gain, voc,
        segment_ids, doc_starts, doc_index, targets,
    )
    return (logprob, like[0], counts[0])


def solution(mesh):
    in_specs = (
        P(("dp", "seq"), "tensor"),
        P(("dp", "seq"), "tensor"),
        P(("dp", "seq"), "tensor"),
        P(None, "tensor"),
        P(("dp", "seq"), "tensor"),
        P("tensor"),
        P("tensor"),
        P(("dp", "seq", "tensor"), None),
        P("dp", "seq"),
        P("dp", None),
        P("dp", None),
        P(),
    )
    out_specs = (P("dp", "seq"), P(), P())
    return jax.shard_map(
        functools.partial(local, mesh), mesh=mesh, in_specs=in_specs, out_specs=out_specs, check_vma=False
    )
```

profile of v0, /device:TPU:0, one launch (start us, length us, event | category | flops | bytes accessed | tf_op | source)
XLA Modules:
  0.0 77.9 jit_solution(3641186465834637422)
XLA Ops:
  0.6 73.9 %packed_loglik.1 = (f32[1,56]{1,0:T(1,128)}, f32[1,32]{1,0:T(1,128)}, f32[1,32]{1,0:T(1,128)}) custom-call(bf16[56,2048]{1,0:T(8,128)(2,1)} %q_ref.1, bf16[56,1024]{1,0:T(8,128)(2,1)} %k_ref.1, bf16[56,1024]{1,0:T(8,128)(2,1)} %v_ref.1, bf16[4096,1792]{1,0:T(8,128)(2,1)} %w_hbm.1, bf16[56,1792]{1,0:T(8,128)(2,1)} %res_ref.1, f32[1792]{0:T(1024)} %pg_ref.1, ...), custom_call_target="tpu_custom_call" | custom-call | tf_op jit(solution)/shard_map/packed_loglik/pallas_call | solution.py:458
  74.5 1.1 %copy.18 = f32[1,56]{1,0:T(1,128)} copy(f32[1,56]{1,0:T(1,128)} %get-tuple-element.12) | data formatting | bytes 448
  75.6 1.1 %copy.19 = f32[32]{0:T(128)} copy(f32[32]{0:T(128)} %bitcast.3) | data formatting | bytes 256
  76.7 1.2 %copy.20 = f32[32]{0:T(128)} copy(f32[32]{0:T(128)} %bitcast.2) | data formatting | bytes 256
where the time goes:
time: 78.1 us; the launch traced here: 77.9 us
  Pallas kernels  73.9 us (95%)
  local copies, waits for them, and re-layouts  3.42 us (4%)
    pallas_call x1, Pallas kernels, local(): pl.pallas_call(functools.partial(body, (ND, NZ, NY, docs)), out_shape=(ja...  73.9 us
    unnamed x3, local copies, waits for them, and re-layouts  3.42 us

commit v1 on v0

v1 whole, which is shorter than its diff:
```python
import functools

import jax
import jax.numpy as jnp
from jax import lax
from jax.experimental import pallas as pl
from jax.experimental.pallas import tpu as pltpu
from jax.sharding import PartitionSpec as P

HEAD_DIM = 256
ATTENTION_CAP = 50.0
LOGIT_CAP = 30.0
EPSILON = 1e-06
MESH = pl.DeviceIdType.MESH
PAD = 64
NT = (((1,), (1,)), ((), ()))
NN = (((1,), (0,)), ((), ()))


def dot(a, b, dims):
    return lax.dot_general(a, b, dims, preferred_element_type=jnp.float32)


def body(
    sizes,
    q_hbm, k_hbm, v_hbm, w_hbm, res_hbm, pg_hbm, fg_hbm, voc_hbm, seg_hbm, start_hbm, index_hbm, target_hbm,
    out_ref,
    q_ref, k_ref, v_ref, res_ref, pg_ref, fg_ref, seg_ref, start_ref, index_ref, target_ref,
    w_ref, voc_ref, kv, num, den, att, branch, stat, hid, held, lab_ref, early_buf, late_buf, twin_buf,
    local_sem, kv_send, kv_recv, att_send, att_recv, st_send, st_recv,
    hid_recv, z_send, y_send, x_send, voc_send, voc_recv, f_send, f_recv, tw_send, tw_recv,
):
    ND, NZ, NY, docs = sizes
    NC = 2 if ND % 2 == 0 else 1
    NX = ND // NC
    D = voc_hbm.shape[-1] if voc_hbm.ndim == 2 else voc_hbm.shape[0] * voc_hbm.shape[2]
    me_d, me_z, me_t = lax.axis_index("dp"), lax.axis_index("seq"), lax.axis_index("tensor")
    me_x, me_c = me_d // NC, me_d % NC
    twin = [me_x * NC + 1 - me_c] if NC == 2 else []
    rows = q_ref.shape[0]
    kvw = k_ref.shape[1]
    groups = kvw // HEAD_DIM
    per = q_ref.shape[1] // kvw
    heads = groups * per
    qw = q_ref.shape[1]
    fw = w_hbm.shape[1]

    pairs = [
        (k_hbm, k_ref), (v_hbm, v_ref), (q_hbm, q_ref), (seg_hbm, seg_ref), (start_hbm, start_ref),
        (index_hbm, index_ref), (target_hbm, target_ref), (res_hbm, res_ref), (pg_hbm, pg_ref), (fg_hbm, fg_ref),
        (w_hbm, w_ref), (voc_hbm, voc_ref.at[me_c]),
    ]
    loads = [pltpu.make_async_copy(src, dst, local_sem.at[i]) for i, (src, dst) in enumerate(pairs)]
    for c in loads:
        c.start()
    w_copy = loads[10]

    def dev(d=None, z=None, t=None):
        return (me_d if d is None else d, me_z if z is None else z, me_t if t is None else t)

    def remote(src, dst, send, recv, device):
        return pltpu.make_async_remote_copy(
            src_ref=src, dst_ref=dst, send_sem=send, recv_sem=recv, device_id=device, device_id_type=MESH
        )

    def others(me, n):
        return [lax.rem(me + i, n) for i in range(1, n)]

    barrier = pltpu.get_barrier_semaphore()
    peers = [dev(d=p * NC + me_c) for p in others(me_x, NX)] + [dev(d=p) for p in twin]
    peers += [dev(t=p) for p in others(me_t, NY)]
    ups = [(me_z + 1 < NZ, dev(z=lax.rem(me_z + 1, NZ))), (me_z >= 1, dev(z=lax.rem(me_z + NZ - 1, NZ)))]
    for p in peers:
        pl.semaphore_signal(barrier, inc=1, device_id=p, device_id_type=MESH)
    for there, p in ups:
        @pl.when(there)
        def _(p=p):
            pl.semaphore_signal(barrier, inc=1, device_id=p, device_id_type=MESH)
    for c in loads[:7]:
        c.wait()

    def kv_copy(block, g):
        cols = pl.ds(g * HEAD_DIM, HEAD_DIM)
        up = dev(z=lax.rem(me_z + 1, NZ))
        if block is None:
            pairs = [(k_ref.at[:, cols], kv.at[me_z, 0, :, cols]), (v_ref.at[:, cols], kv.at[me_z, 1, :, cols])]
            where = me_z
        else:
            pairs = [(kv.at[block, i, :, cols],) * 2 for i in range(2)]
            where = block
        return [
            remote(src, dst, kv_send.at[where, g, i], kv_recv.at[where, g, i], up)
            for i, (src, dst) in enumerate(pairs)
        ]

    seg = seg_ref[...]
    first_row = jnp.zeros((1, rows), jnp.int32)
    end_row = jnp.zeros((1, rows), jnp.int32)
    doc_row = jnp.zeros((1, rows), jnp.int32)
    segs = start_ref.shape[1]
    for n in range(segs):
        here = seg == n
        first_row = jnp.where(here, start_ref[0, n], first_row)
        end_row = jnp.where(here, start_ref[0, n + 1] if n + 1 < segs else rows * NZ, end_row)
        doc_row = jnp.where(here, index_ref[0, n], doc_row)
    spot = me_z * rows + lax.broadcasted_iota(jnp.int32, (1, rows), 1)
    code_row = doc_row + jnp.where(spot + 1 < end_row, docs, 0)
    i_pos = lax.broadcasted_iota(jnp.int32, (rows, rows), 0)
    j_pos = lax.broadcasted_iota(jnp.int32, (rows, rows), 1)

    def column_of(row):
        full = jnp.broadcast_to(row.astype(jnp.float32), (rows, rows))
        return jnp.sum(jnp.where(i_pos == j_pos, full, 0.0), axis=1, keepdims=True)

    first = column_of(first_row).astype(jnp.int32)
    lines = NX * PAD
    lanes = lax.broadcasted_iota(jnp.int32, (rows, lines), 1)
    sub = lax.broadcasted_iota(jnp.int32, (rows, lines), 0)
    placed = jnp.where(lanes == sub + me_x * PAD, column_of(code_row), 0.0)
    code_line = jnp.sum(placed, axis=0, keepdims=True)
    gap = jnp.zeros((1, PAD - rows), jnp.int32)
    for z in range(NZ):
        pieces = []
        for x in range(NX):
            part = target_ref[x * NC:x * NC + 1, z * rows:(z + 1) * rows]
            for c in range(1, NC):
                part = jnp.where(me_c == c, target_ref[x * NC + c:x * NC + c + 1, z * rows:(z + 1) * rows], part)
            pieces += [part, gap]
        lab_ref[z] = jnp.concatenate(pieces, axis=1)

    def attend(block, g):
        cols = slice(g * HEAD_DIM, (g + 1) * HEAD_DIM)
        if block is None:
            kk, vv = k_ref[:, cols], v_ref[:, cols]
            seen = (me_z * rows + j_pos >= first) & (j_pos <= i_pos)
        else:
            kk, vv = kv[block, 0, :, cols], kv[block, 1, :, cols]
            seen = block * rows + j_pos >= first
        for h in range(g * per, (g + 1) * per):
            raw = dot(q_ref[:, h * HEAD_DIM:(h + 1) * HEAD_DIM], kk, NT)
            capped = ATTENTION_CAP * jnp.tanh(raw * (HEAD_DIM ** (-0.5) / ATTENTION_CAP))
            wt = jnp.where(seen, jnp.exp(capped), 0.0)
            top = dot(wt.astype(jnp.bfloat16), vv, NN)
            low = jnp.broadcast_to(jnp.sum(wt, axis=1, keepdims=True), (rows, 128))
            if block is None:
                num[h] = top
                den[h] = low
            else:
                num[h] = num[h] + top
                den[h] = den[h] + low

    def arrived(block, g):
        for c in kv_copy(block, g):
            c.wait_recv()

        @pl.when(me_z + 1 < NZ)
        def _():
            for c in kv_copy(block, g):
                c.start()

    @pl.when(me_z >= 0)
    def _():
        for g in range(groups):
            attend(None, g)

    ends = lax.div(me_z + NZ - 1, NZ) + lax.div(2 * NZ - 2 - me_z, NZ)
    pl.semaphore_wait(barrier, len(peers) + ends)
    @pl.when(me_z + 1 < NZ)
    def _():
        for g in range(groups):
            for c in kv_copy(None, g):
                c.start()
    voc_copies = [
        remote(voc_hbm, voc_ref.at[me_c], voc_send.at[0], voc_recv.at[me_c], dev(d=p)) for p in twin
    ]
    for c in voc_copies:
        c.start()
    for block in range(NZ - 2, 0, -1):
        @pl.when(block < me_z)
        def _(block=block):
            for g in range(groups):
                arrived(block, g)
                attend(block, g)

    gw = per * HEAD_DIM

    def att_copy(g, peer, idx):
        ref = att.at[me_t, :, pl.ds(g * gw, gw)]
        return remote(ref, ref, att_send.at[idx, g], att_recv.at[me_t, g], dev(t=peer))

    step = 256 if fw % 256 == 0 else fw

    def project(t, g, begin):
        base = pl.multiple_of(t * qw + g * gw, gw)
        left = att[t, :, g * gw:(g + 1) * gw]
        for n in range(fw // step):
            cols = slice(n * step, (n + 1) * step)
            got = dot(left, w_ref[pl.ds(base, gw), cols], NN)
            branch[:, cols] = got if begin else branch[:, cols] + got

    for g in range(groups):
        if NZ > 1:
            @pl.when(me_z > 0)
            def _(g=g):
                arrived(0, g)
                attend(0, g)
        for h in range(g * per, (g + 1) * per):
            att[me_t, :, h * HEAD_DIM:(h + 1) * HEAD_DIM] = (num[h] / den[h][:, :1]).astype(jnp.bfloat16)
        for i, p in enumerate(others(me_t, NY)):
            att_copy(g, p, i).start()
        if g == 0:
            w_copy.wait()
        project(me_t, g, g == 0)
    for g in range(groups):
        for p in others(me_t, NY):
            ref = att.at[p, :, pl.ds(g * gw, gw)]
            remote(ref, ref, att_send.at[0, 0], att_recv.at[p, g], dev()).wait_recv()
            project(p, g, False)

    for c in loads[7:10]:
        c.wait()
    br = branch[...]
    carried = res_ref[...].astype(jnp.float32)
    gained = pg_ref[...].reshape(1, fw) * br
    lane = lax.broadcasted_iota(jnp.int32, (rows, 128), 1)
    packed = jnp.zeros((rows, 128), jnp.float32)
    for i, prod in enumerate((br * br, carried * carried, carried * gained, gained * gained)):
        packed = jnp.where(lane == i, jnp.sum(prod, axis=1, keepdims=True), packed)
    stat[me_t] = packed

    def stat_copy(peer, i):
        return remote(stat.at[me_t], stat.at[me_t], st_send.at[i], st_recv.at[me_t], dev(t=peer))

    for i, p in enumerate(others(me_t, NY)):
        stat_copy(p, i).start()
    for p in others(me_t, NY):
        remote(stat.at[p], stat.at[p], st_send.at[0], st_recv.at[p], dev()).wait_recv()
    total = stat[0]
    for t in range(1, NY):
        total = total + stat[t]
    sq_branch, sq_carried, cross, sq_gained = (total[:, i:i + 1] for i in range(4))
    inv_branch = 1.0 / jnp.sqrt(sq_branch / D + EPSILON)
    sq_total = sq_carried + 2.0 * inv_branch * cross + inv_branch * inv_branch * sq_gained
    inv_total = 1.0 / jnp.sqrt(sq_total / D + EPSILON)
    hid[me_z, me_t, me_x, :rows, :] = (
        fg_ref[...].reshape(1, fw) * (carried + gained * inv_branch) * inv_total
    ).astype(jnp.bfloat16)

    y_peers = others(me_t, NY)
    x_peers = others(me_x, NX)
    cut = min(rows, (rows // 2 + 7) // 8 * 8)
    spans = [(0, cut)] + ([(cut, rows - cut)] if cut < rows else [])
    K = len(spans)

    def xdev(x):
        return dev(d=x * NC + me_c)

    def block(z, t, x, k):
        return hid.at[z, t, x, pl.ds(*spans[k]), :]

    def send(z, t, x, k, sem, device):
        return remote(block(z, t, x, k), block(z, t, x, k), sem, hid_recv.at[z, t, x, k], device)

    def landed(z, t, x, k):
        send(z, t, x, k, z_send.at[0, 0, 0], dev()).wait_recv()

    def step_of(n):
        return me_z if n == 0 else jnp.where(n <= me_z, me_z - n, n)

    def spread(n, act, wait):
        z = step_of(n)
        for k in range(K):
            if wait and n > 0:
                landed(z, me_t, me_x, k)

            @pl.when((me_z + 1 < NZ) & (z <= me_z))
            def _(k=k):
                act(send(z, me_t, me_x, k, z_send.at[z, k, 0], dev(z=lax.rem(me_z + 1, NZ))))

            @pl.when((me_z >= 1) & (z >= me_z))
            def _(k=k):
                act(send(z, me_t, me_x, k, z_send.at[z, k, 1], dev(z=lax.rem(me_z + NZ - 1, NZ))))

            for i, p in enumerate(x_peers):
                act(send(z, me_t, me_x, k, x_send.at[0, z, k, i], xdev(p)))
            for i, p in enumerate(y_peers):
                act(send(z, me_t, me_x, k, y_send.at[0, z, k, i], dev(t=p)))

    def relay(n, act, wait):
        z = step_of(n)
        for j, x in enumerate(x_peers):
            if wait:
                landed(z, me_t, x, 0)
            for i, p in enumerate(y_peers):
                act(send(z, me_t, x, 0, y_send.at[1 + j, z, 0, i], dev(t=p)))
        for j, t in enumerate(y_peers):
            if wait:
                landed(z, t, me_x, K - 1)
            if K > 1:
                for i, p in enumerate(x_peers):
                    act(send(z, t, me_x, K - 1, x_send.at[1 + j, z, K - 1, i], xdev(p)))

    def start(c):
        c.start()

    count = voc_hbm.shape[-2]
    home = (me_x * NZ + me_z) * NY + me_t
    row_ids = lax.broadcasted_iota(jnp.int32, (count, lines), 0)

    def product(c, z, t):
        right = hid[z, t].reshape(lines, fw)
        if len(voc_ref.shape) == 3:
            start_col = t * fw if isinstance(t, int) else pl.multiple_of(t * fw, 128)
            left = voc_ref[c, :, pl.ds(start_col, fw)]
        else:
            left = voc_ref[c, t]
        return dot(left, right, NT)

    def gather(z, t, begin):
        @pl.loop(0, NC)
        def _(c):
            got = product(c, z, t)
            held[c] = got if begin else held[c] + got

    def finish(z, t, begin):
        label = lab_ref[z]

        def part(c, sums):
            acc = product(c, z, t)
            if not begin:
                acc = held[c] + acc
            capped = LOGIT_CAP * jnp.tanh(acc * (1.0 / LOGIT_CAP))
            base = (((me_x * NC + c) * NZ + me_z) * NY + me_t) * count
            tot = sums[0] + jnp.sum(jnp.exp(capped), axis=0, keepdims=True)
            cho = sums[1] + jnp.sum(jnp.where(row_ids == label - base, capped, 0.0), axis=0, keepdims=True)
            return tot, cho

        zero = jnp.zeros((1, lines), jnp.float32)
        return lax.fori_loop(0, NC, part, (zero, zero))

    def compute(n, before_last=None):
        z = step_of(n)
        for x in x_peers:
            for k in range(1, K):
                landed(z, me_t, x, k)
        if NY > 1:
            gather(z, me_t, True)
        last = me_t
        for i, t in enumerate(y_peers):
            for k in range(K - 1):
                landed(z, t, me_x, k)
            for x in x_peers:
                for k in range(K):
                    landed(z, t, x, k)
            last = t
            if i + 1 < len(y_peers):
                gather(z, t, False)
        if before_last is not None:
            before_last()
        return z, *finish(z, last, NY == 1)

    family = [(x, z, t) for x in range(NX) for z in range(NZ) for t in range(NY)]
    G = len(family)

    def kin(i):
        other = lax.rem(home + i, G)
        return dev(d=(other // (NZ * NY)) * NC + me_c, z=lax.rem(other // NY, NZ), t=lax.rem(other, NY))

    def early(i):
        return remote(early_buf.at[home], early_buf.at[home], f_send.at[0, i], f_recv.at[0, home], kin(i))

    def late(i):
        return remote(late_buf.at[home], late_buf.at[home], f_send.at[1, i], f_recv.at[1, home], kin(i))

    def send_early():
        for i in range(1, G):
            early(i).start()

    def voc_ready():
        loads[11].wait()
        for p in twin:
            other = lax.rem(p, NC)
            remote(voc_hbm, voc_ref.at[other], voc_send.at[0], voc_recv.at[other], dev()).wait_recv()

    spread(0, start, True)
    relay(0, start, True)
    for n in range(NZ):
        if n + 1 < NZ:
            spread(n + 1, start, True)
            relay(n + 1, start, True)
            if n == 0:
                voc_ready()
            z, tot, cho = compute(n)
            early_buf[home, pl.ds(z, 1), :] = tot
            early_buf[home, pl.ds(NZ + z, 1), :] = cho
        else:
            if n == 0:
                voc_ready()
            early_buf[home, pl.ds(step_of(n), 1), :] = code_line
            early_buf[home, pl.ds(NZ + step_of(n), 1), :] = jnp.zeros((1, lines), jnp.float32)
            z, tot, cho = compute(n, send_early)
            late_buf[home, 0:1, :] = tot
            late_buf[home, 1:2, :] = cho
    for i in range(1, G):
        late(i).start()
    for i in range(1, G):
        other = lax.rem(home + i, G)
        remote(early_buf.at[other], early_buf.at[other], f_send.at[0, 0], f_recv.at[0, other], dev()).wait_recv()
    for i in range(1, G):
        other = lax.rem(home + i, G)
        remote(late_buf.at[other], late_buf.at[other], f_send.at[1, 0], f_recv.at[1, other], dev()).wait_recv()

    def last_of(z):
        return NZ - 1 if z < NZ - 1 else 0

    empty = jnp.zeros((1, lines), jnp.float32)
    totals, chosen, codes = [empty] * NZ, [empty] * NZ, [empty] * NZ
    for i, (x, z, t) in enumerate(family):
        for w in range(NZ):
            if w == last_of(z):
                totals[w] = totals[w] + late_buf[i, 0:1, :]
                chosen[w] = chosen[w] + late_buf[i, 1:2, :]
                if t == 0:
                    codes[z] = codes[z] + early_buf[i, w:w + 1, :]
            else:
                totals[w] = totals[w] + early_buf[i, w:w + 1, :]
                chosen[w] = chosen[w] + early_buf[i, NZ + w:NZ + w + 1, :]
    totals, chosen, code = (jnp.concatenate(p, axis=0) for p in (totals, chosen, codes))
    inside = lax.rem(lax.broadcasted_iota(jnp.int32, (NZ, lines), 1), PAD) < rows
    counted = jnp.where(inside & (code >= docs), 1.0, 0.0)
    doc = jnp.where(code >= docs, code - docs, code)
    logprob = jnp.where(inside, counted * (chosen - jnp.log(totals)), 0.0)
    names = lax.broadcasted_iota(jnp.int32, (docs, lines), 0).astype(jnp.float32)
    like = jnp.zeros((docs, lines), jnp.float32)
    cnt = jnp.zeros((docs, lines), jnp.float32)
    for r in range(NZ):
        hit = names == doc[r:r + 1, :]
        like = like + jnp.where(hit, logprob[r:r + 1, :], 0.0)
        cnt = cnt + jnp.where(hit, counted[r:r + 1, :], 0.0)
    docs_eye = lax.broadcasted_iota(jnp.int32, (docs, 128), 0) == lax.broadcasted_iota(jnp.int32, (docs, 128), 1)
    sums = [
        jnp.sum(jnp.where(docs_eye, jnp.sum(v, axis=1, keepdims=True), 0.0), axis=0, keepdims=True)
        for v in (like, cnt)
    ]
    twin_buf[me_c, 0:1, :] = sums[0]
    twin_buf[me_c, 1:2, :] = sums[1]
    twin_copies = [
        remote(twin_buf.at[me_c], twin_buf.at[me_c], tw_send.at[0], tw_recv.at[me_c], dev(d=p)) for p in twin
    ]
    for c in twin_copies:
        c.start()
    mine = jnp.zeros((1, rows), jnp.float32)
    for z in range(NZ):
        for x in range(NX):
            mine = jnp.where((me_z == z) & (me_x == x), logprob[z:z + 1, x * PAD:x * PAD + rows], mine)
    out_ref[0:1, :rows] = mine
    for i, p in enumerate(others(me_t, NY)):
        for g in range(groups):
            att_copy(g, p, i).wait_send()
        stat_copy(p, i).wait_send()

    def drain(c):
        c.wait_send()

    for n in range(NZ):
        spread(n, drain, False)
        relay(n, drain, False)
    for block in [None, *range(NZ - 1)]:
        @pl.when((me_z + 1 < NZ) if block is None else (me_z > block) & (me_z + 1 < NZ))
        def _(block=block):
            for g in range(groups):
                for c in kv_copy(block, g):
                    c.wait_send()
    for i in range(1, G):
        early(i).wait_send()
        late(i).wait_send()
    for c in voc_copies:
        c.wait_send()
    for p in twin:
        other = lax.rem(p, NC)
        remote(twin_buf.at[other], twin_buf.at[other], tw_send.at[0], tw_recv.at[other], dev()).wait_recv()
    for c in twin_copies:
        c.wait_send()
    both = twin_buf[0]
    for c in range(1, NC):
        both = both + twin_buf[c]
    out_ref[1:3, :] = both


def split(packed, lp_ref, like_ref, cnt_ref):
    lp_ref[...] = packed[0:1, :lp_ref.shape[1]]
    like_ref[...] = packed[1:2, :like_ref.shape[1]]
    cnt_ref[...] = packed[2:3, :cnt_ref.shape[1]]


def local(
    mesh, query_vectors, key_vectors, value_vectors, out_weight, residual, post_gain, final_gain,
    vocab_weight, segment_ids, doc_starts, doc_index, targets,
):
    ND, NZ, NY = mesh.shape["dp"], mesh.shape["seq"], mesh.shape["tensor"]
    rows = query_vectors.shape[0]
    docs = doc_starts.shape[1] * ND
    blocks = ND * NZ
    fw = out_weight.shape[1]
    voc = vocab_weight
    if fw % 128 != 0:
        voc = voc.reshape(voc.shape[0], NY, fw).transpose(1, 0, 2)
    kvw, qw = key_vectors.shape[1], query_vectors.shape[1]
    heads = qw // HEAD_DIM
    groups = kvw // HEAD_DIM
    NC = 2 if ND % 2 == 0 else 1
    NX = ND // NC
    R = blocks * PAD // 128
    f32, bf16, i32 = jnp.float32, jnp.bfloat16, jnp.int32
    dma = pltpu.SemaphoreType.DMA
    lines = NX * PAD
    G = NX * NZ * NY
    anyspace = pl.BlockSpec(memory_space=pl.ANY)
    packed = pl.pallas_call(
        functools.partial(body, (ND, NZ, NY, docs)),
        out_shape=jax.ShapeDtypeStruct((8, 128), f32),
        in_specs=[anyspace] * 12,
        out_specs=pl.BlockSpec(memory_space=pltpu.VMEM),
        scratch_shapes=[
            pltpu.VMEM(query_vectors.shape, bf16),
            pltpu.VMEM(key_vectors.shape, bf16),
            pltpu.VMEM(value_vectors.shape, bf16),
            pltpu.VMEM(residual.shape, bf16),
            pltpu.VMEM(post_gain.shape, f32),
            pltpu.VMEM(final_gain.shape, f32),
            pltpu.VMEM(segment_ids.shape, i32),
            pltpu.SMEM(doc_starts.shape, i32),
            pltpu.SMEM(doc_index.shape, i32),
            pltpu.VMEM(targets.shape, i32),
            pltpu.VMEM(out_weight.shape, bf16),
            pltpu.VMEM((NC, *voc.shape), bf16),
            pltpu.VMEM((NZ, 2, rows, kvw), bf16),
            pltpu.VMEM((heads, rows, HEAD_DIM), f32),
            pltpu.VMEM((heads, rows, 128), f32),
            pltpu.VMEM((NY, rows, qw), bf16),
            pltpu.VMEM((rows, fw), f32),
            pltpu.VMEM((NY, rows, 128), f32),
            pltpu.VMEM((NZ, NY, NX, PAD, fw), bf16),
            pltpu.VMEM((NC, voc.shape[-2], lines), f32),
            pltpu.VMEM((NZ, 1, lines), i32),
            pltpu.VMEM((G, 2 * NZ, lines), f32),
            pltpu.VMEM((G, 2, lines), f32),
            pltpu.VMEM((NC, 2, 128), f32),
            dma((12,)),
            dma((NZ, groups, 2)), dma((NZ, groups, 2)),
            dma((NY, groups)), dma((NY, groups)),
            dma((NY,)), dma((NY,)),
            dma((NZ, NY, NX, 2)),
            dma((NZ, 2, 2)),
            dma((NX, NZ, 2, NY)),
            dma((NY, NZ, 2, NX)),
            dma((1,)), dma((NC,)),
            dma((2, G)), dma((2, G)),
            dma((1,)), dma((NC,)),
        ],
        compiler_params=pltpu.CompilerParams(
            collective_id=0, has_side_effects=True, vmem_limit_bytes=60 * 1024 * 1024
        ),
        name="packed_loglik",
    )(
        query_vectors, key_vectors, value_vectors, out_weight, residual, post_gain, final_gain, voc,
        segment_ids, doc_starts, doc_index, targets,
    )
    sums = jax.ShapeDtypeStruct((1, docs), f32)
    logprob, like, counts = pl.pallas_call(
        split, out_shape=(jax.ShapeDtypeStruct((1, rows), f32), sums, sums), name="split"
    )(packed)
    return (logprob, like[0], counts[0])


def solution(mesh):
    in_specs = (
        P(("dp", "seq"), "tensor"),
        P(("dp", "seq"), "tensor"),
        P(("dp", "seq"), "tensor"),
        P(None, "tensor"),
        P(("dp", "seq"), "tensor"),
        P("tensor"),
        P("tensor"),
        P(("dp", "seq", "tensor"), None),
        P("dp", "seq"),
        P("dp", None),
        P("dp", None),
        P(),
    )
    out_specs = (P("dp", "seq"), P(), P())
    return jax.shard_map(
        functools.partial(local, mesh), mesh=mesh, in_specs=in_specs, out_specs=out_specs, check_vma=False
    )
```

time: 78.1 us -> 73.9 us (0.946)
  local copies, waits for them, and re-layouts: 3.42 us -> 0 us
  Pallas kernels: 73.9 us -> 73.1 us
    unnamed x3 -> x0, local copies, waits for them, and re-layouts: 3.42 us -> none
    pallas_call x1 -> x2, Pallas kernels: 73.9 us -> 73.1 us  [the longest x1 71.9 us: local(): pl.pallas_call(functools.partial(body, (ND, NZ, NY, docs)), out_shape=jax...]
where the time goes in v1:
time: 73.9 us; the launch traced here: 73.8 us
  Pallas kernels  73.1 us (99%)
    pallas_call x1, Pallas kernels, local(): pl.pallas_call(functools.partial(body, (ND, NZ, NY, docs)), out_shape=jax...  71.9 us

profile of v1, /device:TPU:0, one launch (start us, length us, event | category | flops | bytes accessed | tf_op | source)
XLA Modules:
  0.0 73.8 jit_solution(13698593247732517502)
XLA Ops:
  0.6 71.9 %packed_loglik.1.packed = f32[8,128]{1,0:T(8,128)} custom-call(bf16[56,2048]{1,0:T(8,128)(2,1)} %q_hbm.1, bf16[56,1024]{1,0:T(8,128)(2,1)} %k_hbm.1, bf16[56,1024]{1,0:T(8,128)(2,1)} %v_hbm.1, bf16[4096,1792]{1,0:T(8,128)(2,1)} %w_hbm.1, bf16[56,1792]{1,0:T(8,128)(2,1)} %res_hbm.1, f32[1792]{0:T(1024)} %pg_hbm.1, f32[1792]{0:T(1024)} %fg_hbm.1, ...), custom_call_target="tpu_custom_call" | custom-call | tf_op jit(solution)/shard_map/packed_loglik/pallas_call | solution.py:519
  72.6 1.2 %split.1 = (f32[1,56]{1,0:T(1,128)}, f32[1,32]{1,0:T(1,128)}, f32[1,32]{1,0:T(1,128)}) custom-call(f32[8,128]{1,0:T(8,128)} %packed_loglik.1.packed), custom_call_target="tpu_custom_call" | custom-call | tf_op jit(solution)/shard_map/split/pallas_call | solution.py:570

commit v2 on v1

--- a/solution.py
+++ b/solution.py
@@ -28,7 +28,7 @@
     q_ref, k_ref, v_ref, res_ref, pg_ref, fg_ref, seg_ref, start_ref, index_ref, target_ref,
     w_ref, voc_ref, kv, num, den, att, branch, stat, hid, held, lab_ref, early_buf, late_buf, twin_buf,
     local_sem, kv_send, kv_recv, att_send, att_recv, st_send, st_recv,
-    hid_recv, z_send, y_send, x_send, voc_send, voc_recv, f_send, f_recv, tw_send, tw_recv,
+    hid_recv, z_send, d_send, u_send, token, y_send, x_send, voc_send, voc_recv, f_send, f_recv, tw_send, tw_recv,
 ):
     ND, NZ, NY, docs = sizes
     NC = 2 if ND % 2 == 0 else 1
@@ -64,7 +64,7 @@
         )
 
     def others(me, n):
-        return [lax.rem(me + i, n) for i in range(1, n)]
+        return [jnp.where(me + i >= n, me + i - n, me + i) for i in range(1, n)]
 
     barrier = pltpu.get_barrier_semaphore()
     peers = [dev(d=p * NC + me_c) for p in others(me_x, NX)] + [dev(d=p) for p in twin]
@@ -76,7 +76,7 @@
         @pl.when(there)
         def _(p=p):
             pl.semaphore_signal(barrier, inc=1, device_id=p, device_id_type=MESH)
-    for c in loads[:7]:
+    for c in loads[:2]:
         c.wait()
 
     def kv_copy(block, g):
@@ -93,6 +93,20 @@
             for i, (src, dst) in enumerate(pairs)
         ]
 
+    ends = lax.div(me_z + NZ - 1, NZ) + lax.div(2 * NZ - 2 - me_z, NZ)
+    pl.semaphore_wait(barrier, len(peers) + ends)
+    @pl.when(me_z + 1 < NZ)
+    def _():
+        for g in range(groups):
+            for c in kv_copy(None, g):
+                c.start()
+    voc_copies = [
+        remote(voc_hbm, voc_ref.at[me_c], voc_send.at[0], voc_recv.at[me_c], dev(d=p)) for p in twin
+    ]
+    for c in voc_copies:
+        c.start()
+    for c in loads[2:7]:
+        c.wait()
     seg = seg_ref[...]
     first_row = jnp.zeros((1, rows), jnp.int32)
     end_row = jnp.zeros((1, rows), jnp.int32)
@@ -163,18 +177,28 @@
         for g in range(groups):
             attend(None, g)
 
-    ends = lax.div(me_z + NZ - 1, NZ) + lax.div(2 * NZ - 2 - me_z, NZ)
-    pl.semaphore_wait(barrier, len(peers) + ends)
-    @pl.when(me_z + 1 < NZ)
-    def _():
-        for g in range(groups):
-            for c in kv_copy(None, g):
-                c.start()
-    voc_copies = [
-        remote(voc_hbm, voc_ref.at[me_c], voc_send.at[0], voc_recv.at[me_c], dev(d=p)) for p in twin
-    ]
-    for c in voc_copies:
-        c.start()
+    top, bottom = me_z == NZ - 1, me_z == 0
+    under = jnp.logical_not(top) if NZ > 2 else me_z >= 0
+
+    def tell(i, z):
+        pl.semaphore_signal(token.at[i], inc=1, device_id=dev(z=lax.rem(z + NZ, NZ)), device_id_type=MESH)
+
+    if NZ > 1:
+        @pl.when(bottom)
+        def _():
+            tell(0, me_z + 1)
+
+        @pl.when(top)
+        def _():
+            tell(1, me_z - 1)
+
+        @pl.when(jnp.logical_not(bottom | top))
+        def _():
+            pl.semaphore_wait(token.at[1], 1)
+            tell(1, me_z - 1)
+            pl.semaphore_wait(token.at[0], 1)
+            tell(0, me_z + 1)
+
     for block in range(NZ - 2, 0, -1):
         @pl.when(block < me_z)
         def _(block=block):
@@ -262,7 +286,7 @@
         return remote(block(z, t, x, k), block(z, t, x, k), sem, hid_recv.at[z, t, x, k], device)
 
     def landed(z, t, x, k):
-        send(z, t, x, k, z_send.at[0, 0, 0], dev()).wait_recv()
+        send(z, t, x, k, z_send.at[0, 0], dev()).wait_recv()
 
     def step_of(n):
         return me_z if n == 0 else jnp.where(n <= me_z, me_z - n, n)
@@ -272,19 +296,27 @@
         for k in range(K):
             if wait and n > 0:
                 landed(z, me_t, me_x, k)
-
-            @pl.when((me_z + 1 < NZ) & (z <= me_z))
-            def _(k=k):
-                act(send(z, me_t, me_x, k, z_send.at[z, k, 0], dev(z=lax.rem(me_z + 1, NZ))))
-
-            @pl.when((me_z >= 1) & (z >= me_z))
-            def _(k=k):
-                act(send(z, me_t, me_x, k, z_send.at[z, k, 1], dev(z=lax.rem(me_z + NZ - 1, NZ))))
-
             for i, p in enumerate(x_peers):
                 act(send(z, me_t, me_x, k, x_send.at[0, z, k, i], xdev(p)))
             for i, p in enumerate(y_peers):
                 act(send(z, me_t, me_x, k, y_send.at[0, z, k, i], dev(t=p)))
+
+            @pl.when(jnp.logical_not(top) & (z <= me_z))
+            def _(k=k):
+                act(send(z, me_t, me_x, k, z_send.at[z, k], dev(z=lax.rem(me_z + 1, NZ))))
+        if n == 0:
+            for off in range(1, NZ):
+                @pl.when(off <= me_z)
+                def _(off=off):
+                    for k in range(K):
+                        p = lax.rem(me_z + NZ - off, NZ)
+                        act(send(me_z, me_t, me_x, k, d_send.at[off - 1, k], dev(z=p)))
+
+    def lift(act):
+        for j, x in enumerate(x_peers):
+            for i, t in enumerate(y_peers):
+                for k in range(K):
+                    act(send(me_z, t, x, k, u_send.at[j, i, k], dev(z=NZ - 1)))
 
     def relay(n, act, wait):
         z = step_of(n)
@@ -316,19 +348,19 @@
             left = voc_ref[c, t]
         return dot(left, right, NT)
 
-    def gather(z, t, begin):
+    def gather(n, z, t, begin):
         @pl.loop(0, NC)
         def _(c):
             got = product(c, z, t)
-            held[c] = got if begin else held[c] + got
-
-    def finish(z, t, begin):
+            held[n, c] = got if begin else held[n, c] + got
+
+    def finish(n, z, t, begin):
         label = lab_ref[z]
 
         def part(c, sums):
             acc = product(c, z, t)
             if not begin:
-                acc = held[c] + acc
+                acc = held[n, c] + acc
             capped = LOGIT_CAP * jnp.tanh(acc * (1.0 / LOGIT_CAP))
             base = (((me_x * NC + c) * NZ + me_z) * NY + me_t) * count
             tot = sums[0] + jnp.sum(jnp.exp(capped), axis=0, keepdims=True)
@@ -338,13 +370,28 @@
         zero = jnp.zeros((1, lines), jnp.float32)
         return lax.fori_loop(0, NC, part, (zero, zero))
 
-    def compute(n, before_last=None):
+    def begin_slice(n):
         z = step_of(n)
         for x in x_peers:
             for k in range(1, K):
                 landed(z, me_t, x, k)
+        if n > 0 and NZ > 2:
+            @pl.when(top)
+            def _():
+                for x in x_peers:
+                    landed(z, me_t, x, 0)
+        if n == 0:
+            voc_ready()
         if NY > 1:
-            gather(z, me_t, True)
+            gather(n, z, me_t, True)
+
+    def end_slice(n, before_last=None):
+        z = step_of(n)
+        if n > 0 and NZ > 2:
+            @pl.when(top)
+            def _():
+                for t in y_peers:
+                    landed(z, t, me_x, K - 1)
         last = me_t
         for i, t in enumerate(y_peers):
             for k in range(K - 1):
@@ -354,17 +401,27 @@
                     landed(z, t, x, k)
             last = t
             if i + 1 < len(y_peers):
-                gather(z, t, False)
+                gather(n, z, t, False)
         if before_last is not None:
             before_last()
-        return z, *finish(z, last, NY == 1)
+        return z, *finish(n, z, last, NY == 1)
 
     family = [(x, z, t) for x in range(NX) for z in range(NZ) for t in range(NY)]
     G = len(family)
 
+    def wrap(v, n):
+        return jnp.where(v >= n, v - n, v)
+
+    def kin_of(i):
+        return wrap(me_x + i // (NZ * NY), NX), wrap(me_z + i // NY % NZ, NZ), wrap(me_t + i % NY, NY)
+
     def kin(i):
-        other = lax.rem(home + i, G)
-        return dev(d=(other // (NZ * NY)) * NC + me_c, z=lax.rem(other // NY, NZ), t=lax.rem(other, NY))
+        x, z, t = kin_of(i)
+        return dev(d=x * NC + me_c, z=z, t=t)
+
+    def seat(i):
+        x, z, t = kin_of(i)
+        return (x * NZ + z) * NY + t
 
     def early(i):
         return remote(early_buf.at[home], early_buf.at[home], f_send.at[0, i], f_recv.at[0, home], kin(i))
@@ -382,34 +439,87 @@
             other = lax.rem(p, NC)
             remote(voc_hbm, voc_ref.at[other], voc_send.at[0], voc_recv.at[other], dev()).wait_recv()
 
-    spread(0, start, True)
-    relay(0, start, True)
-    for n in range(NZ):
+    def score(n):
         if n + 1 < NZ:
-            spread(n + 1, start, True)
-            relay(n + 1, start, True)
-            if n == 0:
-                voc_ready()
-            z, tot, cho = compute(n)
+            z, tot, cho = end_slice(n)
             early_buf[home, pl.ds(z, 1), :] = tot
             early_buf[home, pl.ds(NZ + z, 1), :] = cho
         else:
-            if n == 0:
-                voc_ready()
             early_buf[home, pl.ds(step_of(n), 1), :] = code_line
             early_buf[home, pl.ds(NZ + step_of(n), 1), :] = jnp.zeros((1, lines), jnp.float32)
-            z, tot, cho = compute(n, send_early)
+            z, tot, cho = end_slice(n, send_early)
             late_buf[home, 0:1, :] = tot
             late_buf[home, 1:2, :] = cho
+
+    if NZ > 1:
+        @pl.when(top)
+        def _():
+            pl.semaphore_wait(token.at[0], 1)
+
+    spread(0, start, True)
+
+    @pl.when(bottom)
+    def _():
+        relay(0, start, True)
+
+    if NZ > 1:
+        @pl.when(bottom)
+        def _():
+            pl.semaphore_wait(token.at[1], 1)
+
+        spread(1, start, True)
+
+        @pl.when(jnp.logical_not(bottom))
+        def _():
+            relay(0, start, True)
+
+    for n in range(2, NZ):
+        @pl.when(n <= me_z)
+        def _(n=n):
+            spread(n, start, True)
+
+    if NZ > 1:
+        @pl.when(under)
+        def _():
+            relay(1, start, True)
+
+    if NZ > 3:
+        @pl.when(me_z == NZ - 2)
+        def _():
+            spread(NZ - 1, start, True)
+
+    for n in range(2, NZ):
+        @pl.when((n > me_z) & ((n < NZ - 1) | (me_z != NZ - 2) | (NZ == 3)))
+        def _(n=n):
+            spread(n, start, True)
+
+        if n == 2:
+            begin_slice(0)
+        else:
+            begin_slice(n - 1)
+        score(n - 2)
+        if n == 2 and NZ > 3:
+            begin_slice(1)
+
+        @pl.when(under)
+        def _(n=n):
+            relay(n, start, True)
+            if n == 2:
+                lift(start)
+
+    if NZ < 3:
+        begin_slice(0)
+    if NZ == 3:
+        begin_slice(1)
+    if NZ > 1:
+        begin_slice(NZ - 1)
+        score(NZ - 2)
+    score(NZ - 1)
     for i in range(1, G):
         late(i).start()
     for i in range(1, G):
-        other = lax.rem(home + i, G)
+        other = seat(i)
         remote(early_buf.at[other], early_buf.at[other], f_send.at[0, 0], f_recv.at[0, other], dev()).wait_recv()
-    for i in range(1, G):
-        other = lax.rem(home + i, G)
-        remote(late_buf.at[other], late_buf.at[other], f_send.at[1, 0], f_recv.at[1, other], dev()).wait_recv()
-
     def last_of(z):
         return NZ - 1 if z < NZ - 1 else 0
 
@@ -417,14 +527,18 @@
     totals, chosen, codes = [empty] * NZ, [empty] * NZ, [empty] * NZ
     for i, (x, z, t) in enumerate(family):
         for w in range(NZ):
-            if w == last_of(z):
-                totals[w] = totals[w] + late_buf[i, 0:1, :]
-                chosen[w] = chosen[w] + late_buf[i, 1:2, :]
-                if t == 0:
-                    codes[z] = codes[z] + early_buf[i, w:w + 1, :]
-            else:
+            if w != last_of(z):
                 totals[w] = totals[w] + early_buf[i, w:w + 1, :]
                 chosen[w] = chosen[w] + early_buf[i, NZ + w:NZ + w + 1, :]
+            elif t == 0:
+                codes[z] = codes[z] + early_buf[i, w:w + 1, :]
+    for i in range(1, G):
+        other = seat(i)
+        remote(late_buf.at[other], late_buf.at[other], f_send.at[1, 0], f_recv.at[1, other], dev()).wait_recv()
+    for i, (x, z, t) in enumerate(family):
+        w = last_of(z)
+        totals[w] = totals[w] + late_buf[i, 0:1, :]
+        chosen[w] = chosen[w] + late_buf[i, 1:2, :]
     totals, chosen, code = (jnp.concatenate(p, axis=0) for p in (totals, chosen, codes))
     inside = lax.rem(lax.broadcasted_iota(jnp.int32, (NZ, lines), 1), PAD) < rows
     counted = jnp.where(inside & (code >= docs), 1.0, 0.0)
@@ -462,9 +576,16 @@
     def drain(c):
         c.wait_send()
 
+    relay(0, drain, False)
     for n in range(NZ):
         spread(n, drain, False)
-        relay(n, drain, False)
+
+    @pl.when(under)
+    def _():
+        if NZ > 2:
+            lift(drain)
+        for n in range(1, NZ):
+            relay(n, drain, False)
     for block in [None, *range(NZ - 1)]:
         @pl.when((me_z + 1 < NZ) if block is None else (me_z > block) & (me_z + 1 < NZ))
         def _(block=block):
@@ -541,7 +662,7 @@
             pltpu.VMEM((rows, fw), f32),
             pltpu.VMEM((NY, rows, 128), f32),
             pltpu.VMEM((NZ, NY, NX, PAD, fw), bf16),
-            pltpu.VMEM((NC, voc.shape[-2], lines), f32),
+            pltpu.VMEM((NZ, NC, voc.shape[-2], lines), f32),
             pltpu.VMEM((NZ, 1, lines), i32),
             pltpu.VMEM((G, 2 * NZ, lines), f32),
             pltpu.VMEM((G, 2, lines), f32),
@@ -551,7 +672,10 @@
             dma((NY, groups)), dma((NY, groups)),
             dma((NY,)), dma((NY,)),
             dma((NZ, NY, NX, 2)),
-            dma((NZ, 2, 2)),
+            dma((NZ, 2)),
+            dma((NZ, 2)),
+            dma((NX, NY, 2)),
+            pltpu.SemaphoreType.REGULAR((2,)),
             dma((NX, NZ, 2, NY)),
             dma((NY, NZ, 2, NX)),
             dma((1,)), dma((NC,)),

time: 73.9 us -> 66.2 us (0.90)
  Pallas kernels: 73.1 us -> 65.4 us
    pallas_call x1, Pallas kernels: 71.9 us -> 64.2 us  [local(): pl.pallas_call(functools.partial(body, (ND, NZ, NY, docs)), out_shape=jax...]
where the time goes in v2:
time: 66.2 us; the launch traced here: 66 us
  Pallas kernels  65.4 us (99%)
    pallas_call x1, Pallas kernels, local(): pl.pallas_call(functools.partial(body, (ND, NZ, NY, docs)), out_shape=jax...  64.2 us

profile of v2, /device:TPU:0, one launch (start us, length us, event | category | flops | bytes accessed | tf_op | source)
XLA Modules:
  0.0 66.0 jit_solution(12501003853691370775)
XLA Ops:
  0.6 64.2 %packed_loglik.1.packed = f32[8,128]{1,0:T(8,128)} custom-call(bf16[56,2048]{1,0:T(8,128)(2,1)} %q_hbm.1, bf16[56,1024]{1,0:T(8,128)(2,1)} %k_hbm.1, bf16[56,1024]{1,0:T(8,128)(2,1)} %v_hbm.1, bf16[4096,1792]{1,0:T(8,128)(2,1)} %w_hbm.1, bf16[56,1792]{1,0:T(8,128)(2,1)} %res_hbm.1, f32[1792]{0:T(1024)} %pg_hbm.1, f32[1792]{0:T(1024)} %fg_hbm.1, ...), custom_call_target="tpu_custom_call" | custom-call | tf_op jit(solution)/shard_map/packed_loglik/pallas_call | solution.py:640
  64.8 1.2 %split.1 = (f32[1,56]{1,0:T(1,128)}, f32[1,32]{1,0:T(1,128)}, f32[1,32]{1,0:T(1,128)}) custom-call(f32[8,128]{1,0:T(8,128)} %packed_loglik.1.packed), custom_call_target="tpu_custom_call" | custom-call | tf_op jit(solution)/shard_map/split/pallas_call | solution.py:694

commit v3 on v2

--- a/solution.py
+++ b/solution.py
@@ -25,7 +25,7 @@
     sizes,
     q_hbm, k_hbm, v_hbm, w_hbm, res_hbm, pg_hbm, fg_hbm, voc_hbm, seg_hbm, start_hbm, index_hbm, target_hbm,
     out_ref,
-    q_ref, k_ref, v_ref, res_ref, pg_ref, fg_ref, seg_ref, start_ref, index_ref, target_ref,
+    q_ref, res_ref, pg_ref, fg_ref, seg_ref, start_ref, index_ref, target_ref,
     w_ref, voc_ref, kv, num, den, att, branch, stat, hid, held, lab_ref, early_buf, late_buf, twin_buf,
     local_sem, kv_send, kv_recv, att_send, att_recv, st_send, st_recv,
     hid_recv, z_send, d_send, u_send, token, y_send, x_send, voc_send, voc_recv, f_send, f_recv, tw_send, tw_recv,
@@ -38,7 +38,7 @@
     me_x, me_c = me_d // NC, me_d % NC
     twin = [me_x * NC + 1 - me_c] if NC == 2 else []
     rows = q_ref.shape[0]
-    kvw = k_ref.shape[1]
+    kvw = k_hbm.shape[1]
     groups = kvw // HEAD_DIM
     per = q_ref.shape[1] // kvw
     heads = groups * per
@@ -46,7 +46,7 @@
     fw = w_hbm.shape[1]
 
     pairs = [
-        (k_hbm, k_ref), (v_hbm, v_ref), (q_hbm, q_ref), (seg_hbm, seg_ref), (start_hbm, start_ref),
+        (k_hbm, kv.at[me_z, 0]), (v_hbm, kv.at[me_z, 1]), (q_hbm, q_ref), (seg_hbm, seg_ref), (start_hbm, start_ref),
         (index_hbm, index_ref), (target_hbm, target_ref), (res_hbm, res_ref), (pg_hbm, pg_ref), (fg_hbm, fg_ref),
         (w_hbm, w_ref), (voc_hbm, voc_ref.at[me_c]),
     ]
@@ -80,26 +80,18 @@
         c.wait()
 
     def kv_copy(block, g):
-        cols = pl.ds(g * HEAD_DIM, HEAD_DIM)
-        up = dev(z=lax.rem(me_z + 1, NZ))
-        if block is None:
-            pairs = [(k_ref.at[:, cols], kv.at[me_z, 0, :, cols]), (v_ref.at[:, cols], kv.at[me_z, 1, :, cols])]
-            where = me_z
-        else:
-            pairs = [(kv.at[block, i, :, cols],) * 2 for i in range(2)]
-            where = block
-        return [
-            remote(src, dst, kv_send.at[where, g, i], kv_recv.at[where, g, i], up)
-            for i, (src, dst) in enumerate(pairs)
-        ]
+        ref = kv.at[block, :, :, pl.ds(g * HEAD_DIM, HEAD_DIM)]
+        return remote(ref, ref, kv_send.at[block], kv_recv.at[block, g], dev(z=lax.rem(me_z + 1, NZ)))
+
+    def kv_sent(block):
+        remote(kv.at[block], kv.at[block], kv_send.at[block], kv_recv.at[block, 0], dev()).wait_send()
 
     ends = lax.div(me_z + NZ - 1, NZ) + lax.div(2 * NZ - 2 - me_z, NZ)
     pl.semaphore_wait(barrier, len(peers) + ends)
     @pl.when(me_z + 1 < NZ)
     def _():
         for g in range(groups):
-            for c in kv_copy(None, g):
-                c.start()
+            kv_copy(me_z, g).start()
     voc_copies = [
         remote(voc_hbm, voc_ref.at[me_c], voc_send.at[0], voc_recv.at[me_c], dev(d=p)) for p in twin
     ]
@@ -131,7 +123,7 @@
     lanes = lax.broadcasted_iota(jnp.int32, (rows, lines), 1)
     sub = lax.broadcasted_iota(jnp.int32, (rows, lines), 0)
     placed = jnp.where(lanes == sub + me_x * PAD, column_of(code_row), 0.0)
-    code_line = jnp.sum(placed, axis=0, keepdims=True)
+    code_line = jnp.sum(placed, axis=0, keepdims=True) * jnp.where(me_t == 0, 1.0, 0.0)
     gap = jnp.zeros((1, PAD - rows), jnp.int32)
     for z in range(NZ):
         pieces = []
@@ -145,7 +137,7 @@
     def attend(block, g):
         cols = slice(g * HEAD_DIM, (g + 1) * HEAD_DIM)
         if block is None:
-            kk, vv = k_ref[:, cols], v_ref[:, cols]
+            kk, vv = kv[me_z, 0, :, cols], kv[me_z, 1, :, cols]
             seen = (me_z * rows + j_pos >= first) & (j_pos <= i_pos)
         else:
             kk, vv = kv[block, 0, :, cols], kv[block, 1, :, cols]
@@ -164,13 +156,11 @@
                 den[h] = den[h] + low
 
     def arrived(block, g):
-        for c in kv_copy(block, g):
-            c.wait_recv()
+        kv_copy(block, g).wait_recv()
 
         @pl.when(me_z + 1 < NZ)
         def _():
-            for c in kv_copy(block, g):
-                c.start()
+            kv_copy(block, g).start()
 
     @pl.when(me_z >= 0)
     def _():
@@ -210,7 +200,7 @@
 
     def att_copy(g, peer, idx):
         ref = att.at[me_t, :, pl.ds(g * gw, gw)]
-        return remote(ref, ref, att_send.at[idx, g], att_recv.at[me_t, g], dev(t=peer))
+        return remote(ref, ref, att_send.at[idx], att_recv.at[me_t, g], dev(t=peer))
 
     step = 256 if fw % 256 == 0 else fw
 
@@ -238,7 +228,7 @@
     for g in range(groups):
         for p in others(me_t, NY):
             ref = att.at[p, :, pl.ds(g * gw, gw)]
-            remote(ref, ref, att_send.at[0, 0], att_recv.at[p, g], dev()).wait_recv()
+            remote(ref, ref, att_send.at[0], att_recv.at[p, g], dev()).wait_recv()
             project(p, g, False)
 
     for c in loads[7:10]:
@@ -286,7 +276,7 @@
         return remote(block(z, t, x, k), block(z, t, x, k), sem, hid_recv.at[z, t, x, k], device)
 
     def landed(z, t, x, k):
-        send(z, t, x, k, z_send.at[0, 0], dev()).wait_recv()
+        send(z, t, x, k, z_send.at[0], dev()).wait_recv()
 
     def step_of(n):
         return me_z if n == 0 else jnp.where(n <= me_z, me_z - n, n)
@@ -297,26 +287,26 @@
             if wait and n > 0:
                 landed(z, me_t, me_x, k)
             for i, p in enumerate(x_peers):
-                act(send(z, me_t, me_x, k, x_send.at[0, z, k, i], xdev(p)))
+                act(send(z, me_t, me_x, k, x_send.at[0, i], xdev(p)))
             for i, p in enumerate(y_peers):
-                act(send(z, me_t, me_x, k, y_send.at[0, z, k, i], dev(t=p)))
+                act(send(z, me_t, me_x, k, y_send.at[0, i], dev(t=p)))
 
             @pl.when(jnp.logical_not(top) & (z <= me_z))
             def _(k=k):
-                act(send(z, me_t, me_x, k, z_send.at[z, k], dev(z=lax.rem(me_z + 1, NZ))))
+                act(send(z, me_t, me_x, k, z_send.at[z], dev(z=lax.rem(me_z + 1, NZ))))
         if n == 0:
             for off in range(1, NZ):
                 @pl.when(off <= me_z)
                 def _(off=off):
                     for k in range(K):
                         p = lax.rem(me_z + NZ - off, NZ)
-                        act(send(me_z, me_t, me_x, k, d_send.at[off - 1, k], dev(z=p)))
+                        act(send(me_z, me_t, me_x, k, d_send.at[off - 1], dev(z=p)))
 
     def lift(act):
         for j, x in enumerate(x_peers):
             for i, t in enumerate(y_peers):
                 for k in range(K):
-                    act(send(me_z, t, x, k, u_send.at[j, i, k], dev(z=NZ - 1)))
+                    act(send(me_z, t, x, k, u_send.at[j, i], dev(z=NZ - 1)))
 
     def relay(n, act, wait):
         z = step_of(n)
@@ -324,13 +314,13 @@
             if wait:
                 landed(z, me_t, x, 0)
             for i, p in enumerate(y_peers):
-                act(send(z, me_t, x, 0, y_send.at[1 + j, z, 0, i], dev(t=p)))
+                act(send(z, me_t, x, 0, y_send.at[1 + j, i], dev(t=p)))
         for j, t in enumerate(y_peers):
             if wait:
                 landed(z, t, me_x, K - 1)
             if K > 1:
                 for i, p in enumerate(x_peers):
-                    act(send(z, t, me_x, K - 1, x_send.at[1 + j, z, K - 1, i], xdev(p)))
+                    act(send(z, t, me_x, K - 1, x_send.at[1 + j, i], xdev(p)))
 
     def start(c):
         c.start()
@@ -419,15 +409,11 @@
         x, z, t = kin_of(i)
         return dev(d=x * NC + me_c, z=z, t=t)
 
-    def seat(i):
-        x, z, t = kin_of(i)
-        return (x * NZ + z) * NY + t
-
     def early(i):
-        return remote(early_buf.at[home], early_buf.at[home], f_send.at[0, i], f_recv.at[0, home], kin(i))
+        return remote(early_buf.at[home], early_buf.at[home], f_send.at[0], f_recv.at[0], kin(i))
 
     def late(i):
-        return remote(late_buf.at[home], late_buf.at[home], f_send.at[1, i], f_recv.at[1, home], kin(i))
+        return remote(late_buf.at[home], late_buf.at[home], f_send.at[1], f_recv.at[1], kin(i))
 
     def send_early():
         for i in range(1, G):
@@ -517,28 +503,40 @@
     score(NZ - 1)
     for i in range(1, G):
         late(i).start()
-    for i in range(1, G):
-        other = seat(i)
-        remote(early_buf.at[other], early_buf.at[other], f_send.at[0, 0], f_recv.at[0, other], dev()).wait_recv()
+    def others_of(buf, k):
+        ref = buf.at[pl.ds(0, G - 1)]
+        return remote(ref, ref, f_send.at[k], f_recv.at[k], dev())
+
+    if G > 1:
+        others_of(early_buf, 0).wait_recv()
+
     def last_of(z):
         return NZ - 1 if z < NZ - 1 else 0
 
+    def summed(buf, z):
+        out = None
+        for x in range(NX):
+            for t in range(NY):
+                part = buf[(x * NZ + z) * NY + t]
+                out = part if out is None else out + part
+        return out
+
     empty = jnp.zeros((1, lines), jnp.float32)
     totals, chosen, codes = [empty] * NZ, [empty] * NZ, [empty] * NZ
-    for i, (x, z, t) in enumerate(family):
+    for z in range(NZ):
+        sums = summed(early_buf, z)
         for w in range(NZ):
-            if w != last_of(z):
-                totals[w] = totals[w] + early_buf[i, w:w + 1, :]
-                chosen[w] = chosen[w] + early_buf[i, NZ + w:NZ + w + 1, :]
-            elif t == 0:
-                codes[z] = codes[z] + early_buf[i, w:w + 1, :]
-    for i in range(1, G):
-        other = seat(i)
-        remote(late_buf.at[other], late_buf.at[other], f_send.at[1, 0], f_recv.at[1, other], dev()).wait_recv()
-    for i, (x, z, t) in enumerate(family):
-        w = last_of(z)
-        totals[w] = totals[w] + late_buf[i, 0:1, :]
-        chosen[w] = chosen[w] + late_buf[i, 1:2, :]
+            if w == last_of(z):
+                codes[z] = sums[w:w + 1]
+            else:
+                totals[w] = totals[w] + sums[w:w + 1]
+                chosen[w] = chosen[w] + sums[NZ + w:NZ + w + 1]
+    if G > 1:
+        others_of(late_buf, 1).wait_recv()
+    for z in range(NZ):
+        sums = summed(late_buf, z)
+        totals[last_of(z)] = totals[last_of(z)] + sums[0:1]
+        chosen[last_of(z)] = chosen[last_of(z)] + sums[1:2]
     totals, chosen, code = (jnp.concatenate(p, axis=0) for p in (totals, chosen, codes))
     inside = lax.rem(lax.broadcasted_iota(jnp.int32, (NZ, lines), 1), PAD) < rows
     counted = jnp.where(inside & (code >= docs), 1.0, 0.0)
@@ -569,32 +567,58 @@
             mine = jnp.where((me_z == z) & (me_x == x), logprob[z:z + 1, x * PAD:x * PAD + rows], mine)
     out_ref[0:1, :rows] = mine
     for i, p in enumerate(others(me_t, NY)):
-        for g in range(groups):
-            att_copy(g, p, i).wait_send()
+        remote(att.at[me_t], att.at[me_t], att_send.at[i], att_recv.at[me_t, 0], dev()).wait_send()
         stat_copy(p, i).wait_send()
 
-    def drain(c):
-        c.wait_send()
-
-    relay(0, drain, False)
-    for n in range(NZ):
-        spread(n, drain, False)
+    def sent(ref, sem):
+        remote(ref, ref, sem, hid_recv.at[0, 0, 0, 0], dev()).wait_send()
+
+    def portion(k, n):
+        return hid.at[pl.ds(0, n), 0, 0, pl.ds(*k), :]
+
+    whole = (0, rows)
+    for i in range(len(x_peers)):
+        sent(portion(whole, NZ), x_send.at[0, i])
+    for i in range(len(y_peers)):
+        sent(portion(whole, NZ), y_send.at[0, i])
+
+    def relays_sent(n):
+        for j in range(len(x_peers)):
+            for i in range(len(y_peers)):
+                sent(portion(spans[0], n), y_send.at[1 + j, i])
+        for j in range(len(y_peers)):
+            if K > 1:
+                for i in range(len(x_peers)):
+                    sent(portion(spans[K - 1], n), x_send.at[1 + j, i])
 
     @pl.when(under)
     def _():
+        relays_sent(NZ)
         if NZ > 2:
-            lift(drain)
-        for n in range(1, NZ):
-            relay(n, drain, False)
-    for block in [None, *range(NZ - 1)]:
-        @pl.when((me_z + 1 < NZ) if block is None else (me_z > block) & (me_z + 1 < NZ))
+            for j in range(len(x_peers)):
+                for i in range(len(y_peers)):
+                    sent(portion(whole, 1), u_send.at[j, i])
+
+    if NZ > 2:
+        @pl.when(top)
+        def _():
+            relays_sent(1)
+
+    for z in range(NZ - 1):
+        @pl.when(jnp.logical_not(top) & (z <= me_z))
+        def _(z=z):
+            sent(portion(whole, 1), z_send.at[z])
+
+        @pl.when(z < me_z)
+        def _(z=z):
+            sent(portion(whole, 1), d_send.at[z])
+    for block in range(NZ - 1):
+        @pl.when((me_z >= block) & (me_z + 1 < NZ))
         def _(block=block):
-            for g in range(groups):
-                for c in kv_copy(block, g):
-                    c.wait_send()
-    for i in range(1, G):
-        early(i).wait_send()
-        late(i).wait_send()
+            kv_sent(block)
+    if G > 1:
+        others_of(early_buf, 0).wait_send()
+        others_of(late_buf, 1).wait_send()
     for c in voc_copies:
         c.wait_send()
     for p in twin:
@@ -644,8 +668,6 @@
         out_specs=pl.BlockSpec(memory_space=pltpu.VMEM),
         scratch_shapes=[
             pltpu.VMEM(query_vectors.shape, bf16),
-            pltpu.VMEM(key_vectors.shape, bf16),
-            pltpu.VMEM(value_vectors.shape, bf16),
             pltpu.VMEM(residual.shape, bf16),
             pltpu.VMEM(post_gain.shape, f32),
             pltpu.VMEM(final_gain.shape, f32),
@@ -668,18 +690,18 @@
             pltpu.VMEM((G, 2, lines), f32),
             pltpu.VMEM((NC, 2, 128), f32),
             dma((12,)),
-            dma((NZ, groups, 2)), dma((NZ, groups, 2)),
-            dma((NY, groups)), dma((NY, groups)),
+            dma((NZ,)), dma((NZ, groups)),
+            dma((NY,)), dma((NY, groups)),
             dma((NY,)), dma((NY,)),
             dma((NZ, NY, NX, 2)),
-            dma((NZ, 2)),
-            dma((NZ, 2)),
-            dma((NX, NY, 2)),
+            dma((NZ,)),
+            dma((NZ,)),
+            dma((NX, NY)),
             pltpu.SemaphoreType.REGULAR((2,)),
-            dma((NX, NZ, 2, NY)),
-            dma((NY, NZ, 2, NX)),
+            dma((NX, NY)),
+            dma((NY, NX)),
             dma((1,)), dma((NC,)),
-            dma((2, G)), dma((2, G)),
+            dma((2,)), dma((2,)),
             dma((1,)), dma((NC,)),
         ],
         compiler_params=pltpu.CompilerParams(

time: 66.2 us -> 64.6 us (0.976)
  Pallas kernels: 65.4 us -> 63.8 us
    pallas_call x1, Pallas kernels: 64.2 us -> 62.6 us  [local(): pl.pallas_call(functools.partial(body, (ND, NZ, NY, docs)), out_shape=jax...]
where the time goes in v3:
time: 64.6 us; the launch traced here: 64.4 us
  Pallas kernels  63.8 us (99%)
    pallas_call x1, Pallas kernels, local(): pl.pallas_call(functools.partial(body, (ND, NZ, NY, docs)), out_shape=jax...  62.6 us

profile of v3, /device:TPU:0, one launch (start us, length us, event | category | flops | bytes accessed | tf_op | source)
XLA Modules:
  0.0 64.4 jit_solution(14702460591248434292)
XLA Ops:
  0.6 62.6 %packed_loglik.1.packed = f32[8,128]{1,0:T(8,128)} custom-call(bf16[56,2048]{1,0:T(8,128)(2,1)} %q_hbm.1, bf16[56,1024]{1,0:T(8,128)(2,1)} %k_hbm.1, bf16[56,1024]{1,0:T(8,128)(2,1)} %v_hbm.1, bf16[4096,1792]{1,0:T(8,128)(2,1)} %w_hbm.1, bf16[56,1792]{1,0:T(8,128)(2,1)} %res_hbm.1, f32[1792]{0:T(1024)} %pg_hbm.1, f32[1792]{0:T(1024)} %fg_hbm.1, ...), custom_call_target="tpu_custom_call" | custom-call | tf_op jit(solution)/shard_map/packed_loglik/pallas_call | solution.py:664
  63.2 1.2 %split.1 = (f32[1,56]{1,0:T(1,128)}, f32[1,32]{1,0:T(1,128)}, f32[1,32]{1,0:T(1,128)}) custom-call(f32[8,128]{1,0:T(8,128)} %packed_loglik.1.packed), custom_call_target="tpu_custom_call" | custom-call | tf_op jit(solution)/shard_map/split/pallas_call | solution.py:716

commit v4 on v3

--- a/solution.py
+++ b/solution.py
@@ -25,9 +25,9 @@
     sizes,
     q_hbm, k_hbm, v_hbm, w_hbm, res_hbm, pg_hbm, fg_hbm, voc_hbm, seg_hbm, start_hbm, index_hbm, target_hbm,
     out_ref,
-    q_ref, res_ref, pg_ref, fg_ref, seg_ref, start_ref, index_ref, target_ref,
+    q_ref, top_first, over, under_sum, res_ref, pg_ref, fg_ref, seg_ref, start_ref, index_ref, target_ref,
     w_ref, voc_ref, kv, num, den, att, branch, stat, hid, held, lab_ref, early_buf, late_buf, twin_buf,
-    local_sem, kv_send, kv_recv, att_send, att_recv, st_send, st_recv,
+    local_sem, q_send, q_recv, o_send, o_recv, kv_send, kv_recv, att_send, att_recv, st_send, st_recv,
     hid_recv, z_send, d_send, u_send, token, y_send, x_send, voc_send, voc_recv, f_send, f_recv, tw_send, tw_recv,
 ):
     ND, NZ, NY, docs = sizes
@@ -37,16 +37,16 @@
     me_d, me_z, me_t = lax.axis_index("dp"), lax.axis_index("seq"), lax.axis_index("tensor")
     me_x, me_c = me_d // NC, me_d % NC
     twin = [me_x * NC + 1 - me_c] if NC == 2 else []
-    rows = q_ref.shape[0]
+    rows = q_hbm.shape[0]
     kvw = k_hbm.shape[1]
     groups = kvw // HEAD_DIM
-    per = q_ref.shape[1] // kvw
+    per = q_hbm.shape[1] // kvw
     heads = groups * per
-    qw = q_ref.shape[1]
+    qw = q_hbm.shape[1]
     fw = w_hbm.shape[1]
 
     pairs = [
-        (k_hbm, kv.at[me_z, 0]), (v_hbm, kv.at[me_z, 1]), (q_hbm, q_ref), (seg_hbm, seg_ref), (start_hbm, start_ref),
+        (k_hbm, kv.at[me_z, 0]), (v_hbm, kv.at[me_z, 1]), (q_hbm, q_ref.at[0]), (seg_hbm, seg_ref.at[0]), (start_hbm, start_ref),
         (index_hbm, index_ref), (target_hbm, target_ref), (res_hbm, res_ref), (pg_hbm, pg_ref), (fg_hbm, fg_ref),
         (w_hbm, w_ref), (voc_hbm, voc_ref.at[me_c]),
     ]
@@ -88,7 +88,7 @@
 
     ends = lax.div(me_z + NZ - 1, NZ) + lax.div(2 * NZ - 2 - me_z, NZ)
     pl.semaphore_wait(barrier, len(peers) + ends)
-    @pl.when(me_z + 1 < NZ)
+    @pl.when(me_z < NZ - 2)
     def _():
         for g in range(groups):
             kv_copy(me_z, g).start()
@@ -99,7 +99,13 @@
         c.start()
     for c in loads[2:7]:
         c.wait()
-    seg = seg_ref[...]
+    def first_of(seg):
+        out = jnp.zeros((1, rows), jnp.int32)
+        for n in range(start_ref.shape[1]):
+            out = jnp.where(seg == n, start_ref[0, n], out)
+        return out
+
+    seg = seg_ref[0]
     first_row = jnp.zeros((1, rows), jnp.int32)
     end_row = jnp.zeros((1, rows), jnp.int32)
     doc_row = jnp.zeros((1, rows), jnp.int32)
@@ -119,6 +125,33 @@
         return jnp.sum(jnp.where(i_pos == j_pos, full, 0.0), axis=1, keepdims=True)
 
     first = column_of(first_row).astype(jnp.int32)
+    top, bottom, helper = me_z == NZ - 1, me_z == 0, me_z == NZ - 2
+    gw = per * HEAD_DIM
+
+    def query_copy(g):
+        cols = pl.ds(g * gw, gw)
+        return remote(
+            q_ref.at[0, :, cols], q_ref.at[1, :, cols], q_send.at[0], q_recv.at[g], dev(z=lax.rem(me_z + NZ - 1, NZ))
+        )
+
+    def segment_copy():
+        return remote(seg_ref.at[0], seg_ref.at[1], q_send.at[1], q_recv.at[groups], dev(z=lax.rem(me_z + NZ - 1, NZ)))
+
+    def part_copies(g):
+        cols = pl.ds(g * gw, gw)
+        above = dev(z=lax.rem(me_z + 1, NZ))
+        return [
+            remote(over.at[:, cols], over.at[:, cols], o_send.at[0], o_recv.at[0, g], above),
+            remote(under_sum.at[g], under_sum.at[g], o_send.at[1], o_recv.at[1, g], above),
+        ]
+
+    if NZ > 1:
+        @pl.when(top)
+        def _():
+            segment_copy().start()
+            for g in range(groups):
+                query_copy(g).start()
+
     lines = NX * PAD
     lanes = lax.broadcasted_iota(jnp.int32, (rows, lines), 1)
     sub = lax.broadcasted_iota(jnp.int32, (rows, lines), 0)
@@ -134,40 +167,51 @@
             pieces += [part, gap]
         lab_ref[z] = jnp.concatenate(pieces, axis=1)
 
-    def attend(block, g):
+    def attend(g, *jobs):
         cols = slice(g * HEAD_DIM, (g + 1) * HEAD_DIM)
-        if block is None:
-            kk, vv = kv[me_z, 0, :, cols], kv[me_z, 1, :, cols]
-            seen = (me_z * rows + j_pos >= first) & (j_pos <= i_pos)
-        else:
-            kk, vv = kv[block, 0, :, cols], kv[block, 1, :, cols]
-            seen = block * rows + j_pos >= first
-        for h in range(g * per, (g + 1) * per):
-            raw = dot(q_ref[:, h * HEAD_DIM:(h + 1) * HEAD_DIM], kk, NT)
+        span = range(g * per, (g + 1) * per)
+        raws, parts = [], {}
+        for who, block in jobs:
+            kk = kv[me_z if block is None else block, 0, :, cols]
+            for h in span:
+                raws.append(dot(q_ref[who, :, h * HEAD_DIM:(h + 1) * HEAD_DIM], kk, NT))
+        wts = []
+        for i, raw in enumerate(raws):
+            who, block = jobs[i // per]
+            if block is None:
+                seen = (me_z * rows + j_pos >= first) & (j_pos <= i_pos)
+            else:
+                seen = block * rows + j_pos >= (first if who == 0 else top_first[:, :1])
             capped = ATTENTION_CAP * jnp.tanh(raw * (HEAD_DIM ** (-0.5) / ATTENTION_CAP))
-            wt = jnp.where(seen, jnp.exp(capped), 0.0)
-            top = dot(wt.astype(jnp.bfloat16), vv, NN)
+            wts.append(jnp.where(seen, jnp.exp(capped), 0.0))
+        for i, wt in enumerate(wts):
+            who, block = jobs[i // per]
+            vv = kv[me_z if block is None else block, 1, :, cols]
+            up = dot(wt.astype(jnp.bfloat16), vv, NN)
             low = jnp.broadcast_to(jnp.sum(wt, axis=1, keepdims=True), (rows, 128))
-            if block is None:
-                num[h] = top
-                den[h] = low
+            at = who * heads + span[i % per]
+            if at in parts:
+                parts[at] = (parts[at][0] + up, parts[at][1] + low)
+            elif who == 0 and block is not None:
+                parts[at] = (num[at] + up, den[at] + low)
             else:
-                num[h] = num[h] + top
-                den[h] = den[h] + low
+                parts[at] = (up, low)
+        for at, (up, low) in parts.items():
+            num[at] = up
+            den[at] = low
 
     def arrived(block, g):
         kv_copy(block, g).wait_recv()
 
-        @pl.when(me_z + 1 < NZ)
+        @pl.when(me_z < NZ - 2)
         def _():
             kv_copy(block, g).start()
 
     @pl.when(me_z >= 0)
     def _():
         for g in range(groups):
-            attend(None, g)
-
-    top, bottom = me_z == NZ - 1, me_z == 0
+            attend(g, (0, None))
+
     under = jnp.logical_not(top) if NZ > 2 else me_z >= 0
 
     def tell(i, z):
@@ -189,15 +233,19 @@
             pl.semaphore_wait(token.at[0], 1)
             tell(0, me_z + 1)
 
-    for block in range(NZ - 2, 0, -1):
-        @pl.when(block < me_z)
+    for block in range(NZ - 3, 0, -1):
+        @pl.when((block < me_z) & jnp.logical_not(top))
         def _(block=block):
             for g in range(groups):
                 arrived(block, g)
-                attend(block, g)
-
-    gw = per * HEAD_DIM
-
+                attend(g, (0, block))
+
+    if NZ > 1:
+        @pl.when(helper)
+        def _():
+            segment_copy().wait_recv()
+            top_first[...] = jnp.broadcast_to(column_of(first_of(seg_ref[1])).astype(jnp.int32), (rows, 128))
+            under_sum[...] = jnp.zeros(under_sum.shape, jnp.float32)
     def att_copy(g, peer, idx):
         ref = att.at[me_t, :, pl.ds(g * gw, gw)]
         return remote(ref, ref, att_send.at[idx], att_recv.at[me_t, g], dev(t=peer))
@@ -214,14 +262,44 @@
 
     for g in range(groups):
         if NZ > 1:
-            @pl.when(me_z > 0)
+            @pl.when((me_z > 0) & jnp.logical_not(top | helper))
             def _(g=g):
                 arrived(0, g)
-                attend(0, g)
+                attend(g, (0, 0))
+
+            @pl.when(helper)
+            def _(g=g):
+                query_copy(g).wait_recv()
+                if NZ > 2:
+                    arrived(0, g)
+                    attend(g, (0, 0), *[(1, block) for block in range(NZ - 1)])
+                else:
+                    attend(g, (1, 0))
+
+            @pl.when(top)
+            def _(g=g):
+                for c in part_copies(g):
+                    c.wait_recv()
+                for h in range(g * per, (g + 1) * per):
+                    num[h] = num[h] + over[:, h * HEAD_DIM:(h + 1) * HEAD_DIM].astype(jnp.float32)
+                    r = h - g * per
+                    den[h] = den[h] + jnp.broadcast_to(column_of(under_sum[g, r:r + 1, :rows]), (rows, 128))
+
         for h in range(g * per, (g + 1) * per):
             att[me_t, :, h * HEAD_DIM:(h + 1) * HEAD_DIM] = (num[h] / den[h][:, :1]).astype(jnp.bfloat16)
         for i, p in enumerate(others(me_t, NY)):
             att_copy(g, p, i).start()
+        if NZ > 1:
+            @pl.when(helper)
+            def _(g=g):
+                for h in range(g * per, (g + 1) * per):
+                    over[:, h * HEAD_DIM:(h + 1) * HEAD_DIM] = num[heads + h].astype(jnp.bfloat16)
+                    wide = jnp.broadcast_to(den[heads + h][:, :1], (rows, rows))
+                    r = h - g * per
+                    under_sum[g, r:r + 1, :rows] = jnp.sum(jnp.where(i_pos == j_pos, wide, 0.0), axis=0, keepdims=True)
+                for c in part_copies(g):
+                    c.start()
+
         if g == 0:
             w_copy.wait()
         project(me_t, g, g == 0)
@@ -279,7 +357,17 @@
         send(z, t, x, k, z_send.at[0], dev()).wait_recv()
 
     def step_of(n):
-        return me_z if n == 0 else jnp.where(n <= me_z, me_z - n, n)
+        if n == 0:
+            return me_z
+        out = jnp.where(n <= me_z, me_z - n, n)
+        return jnp.where(top, 0 if n == 1 else me_z - n + 1, out) if NZ > 2 else out
+
+    def climbs(z):
+        up = jnp.logical_not(top) & (z <= me_z)
+        return up & jnp.logical_not(helper & (z == 0)) if NZ > 2 else up
+
+    def falls(z):
+        return (me_z > 0) & (z > me_z) & (z < NZ - 1)
 
     def spread(n, act, wait):
         z = step_of(n)
@@ -291,12 +379,22 @@
             for i, p in enumerate(y_peers):
                 act(send(z, me_t, me_x, k, y_send.at[0, i], dev(t=p)))
 
-            @pl.when(jnp.logical_not(top) & (z <= me_z))
+            if n > 0:
+                @pl.when(falls(z))
+                def _(k=k):
+                    act(send(z, me_t, me_x, k, d_send.at[z], dev(z=lax.rem(me_z + NZ - 1, NZ))))
+
+            @pl.when(climbs(z))
             def _(k=k):
                 act(send(z, me_t, me_x, k, z_send.at[z], dev(z=lax.rem(me_z + 1, NZ))))
+        if n == 0 and NZ > 2:
+            @pl.when(bottom)
+            def _():
+                for k in range(K):
+                    act(send(me_z, me_t, me_x, k, z_send.at[NZ - 1], dev(z=NZ - 1)))
         if n == 0:
             for off in range(1, NZ):
-                @pl.when(off <= me_z)
+                @pl.when((off <= me_z) & (top | (off == 1)))
                 def _(off=off):
                     for k in range(K):
                         p = lax.rem(me_z + NZ - off, NZ)
@@ -442,6 +540,10 @@
         def _():
             pl.semaphore_wait(token.at[0], 1)
 
+        @pl.when(bottom)
+        def _():
+            pl.semaphore_wait(token.at[1], 1)
+
     spread(0, start, True)
 
     @pl.when(bottom)
@@ -449,10 +551,6 @@
         relay(0, start, True)
 
     if NZ > 1:
-        @pl.when(bottom)
-        def _():
-            pl.semaphore_wait(token.at[1], 1)
-
         spread(1, start, True)
 
         @pl.when(jnp.logical_not(bottom))
@@ -489,9 +587,9 @@
 
         @pl.when(under)
         def _(n=n):
-            relay(n, start, True)
             if n == 2:
                 lift(start)
+            relay(n, start, True)
 
     if NZ < 3:
         begin_slice(0)
@@ -511,7 +609,7 @@
         others_of(early_buf, 0).wait_recv()
 
     def last_of(z):
-        return NZ - 1 if z < NZ - 1 else 0
+        return NZ - 1 if z < NZ - 1 else min(1, max(NZ - 2, 0))
 
     def summed(buf, z):
         out = None
@@ -600,20 +698,35 @@
                     sent(portion(whole, 1), u_send.at[j, i])
 
     if NZ > 2:
+        @pl.when(bottom)
+        def _():
+            sent(portion(whole, 1), z_send.at[NZ - 1])
+
         @pl.when(top)
         def _():
             relays_sent(1)
 
     for z in range(NZ - 1):
-        @pl.when(jnp.logical_not(top) & (z <= me_z))
+        @pl.when(climbs(z))
         def _(z=z):
             sent(portion(whole, 1), z_send.at[z])
 
-        @pl.when(z < me_z)
+        @pl.when(((z < me_z) & (top | (z == 0))) | falls(z))
         def _(z=z):
             sent(portion(whole, 1), d_send.at[z])
-    for block in range(NZ - 1):
-        @pl.when((me_z >= block) & (me_z + 1 < NZ))
+    if NZ > 1:
+        @pl.when(top)
+        def _():
+            segment_copy().wait_send()
+            remote(q_ref.at[0], q_ref.at[1], q_send.at[0], q_recv.at[0], dev()).wait_send()
+
+        @pl.when(helper)
+        def _():
+            remote(over, over, o_send.at[0], o_recv.at[0, 0], dev()).wait_send()
+            remote(under_sum, under_sum, o_send.at[1], o_recv.at[1, 0], dev()).wait_send()
+
+    for block in range(NZ - 2):
+        @pl.when((me_z >= block) & (me_z < NZ - 2))
         def _(block=block):
             kv_sent(block)
     if G > 1:
@@ -667,19 +780,22 @@
         in_specs=[anyspace] * 12,
         out_specs=pl.BlockSpec(memory_space=pltpu.VMEM),
         scratch_shapes=[
+            pltpu.VMEM((2, *query_vectors.shape), bf16),
+            pltpu.VMEM((rows, 128), i32),
             pltpu.VMEM(query_vectors.shape, bf16),
+            pltpu.VMEM((groups, 8, 128), f32),
             pltpu.VMEM(residual.shape, bf16),
             pltpu.VMEM(post_gain.shape, f32),
             pltpu.VMEM(final_gain.shape, f32),
-            pltpu.VMEM(segment_ids.shape, i32),
+            pltpu.VMEM((2, *segment_ids.shape), i32),
             pltpu.SMEM(doc_starts.shape, i32),
             pltpu.SMEM(doc_index.shape, i32),
             pltpu.VMEM(targets.shape, i32),
             pltpu.VMEM(out_weight.shape, bf16),
             pltpu.VMEM((NC, *voc.shape), bf16),
             pltpu.VMEM((NZ, 2, rows, kvw), bf16),
-            pltpu.VMEM((heads, rows, HEAD_DIM), f32),
-            pltpu.VMEM((heads, rows, 128), f32),
+            pltpu.VMEM((2 * heads, rows, HEAD_DIM), f32),
+            pltpu.VMEM((2 * heads, rows, 128), f32),
             pltpu.VMEM((NY, rows, qw), bf16),
             pltpu.VMEM((rows, fw), f32),
             pltpu.VMEM((NY, rows, 128), f32),
@@ -690,6 +806,8 @@
             pltpu.VMEM((G, 2, lines), f32),
             pltpu.VMEM((NC, 2, 128), f32),
             dma((12,)),
+            dma((2,)), dma((groups + 1,)),
+            dma((2,)), dma((2, groups)),
             dma((NZ,)), dma((NZ, groups)),
             dma((NY,)), dma((NY, groups)),
             dma((NY,)), dma((NY,)),

time: 64.6 us -> 62.3 us (0.964)
  Pallas kernels: 63.8 us -> 61.4 us
    pallas_call x1, Pallas kernels: 62.6 us -> 60.2 us  [local(): pl.pallas_call(functools.partial(body, (ND, NZ, NY, docs)), out_shape=jax...]
where the time goes in v4:
time: 62.3 us; the launch traced here: 62.1 us
  Pallas kernels  61.4 us (99%)
  between operations  0.64 us (1%)
    pallas_call x1, Pallas kernels, local(): pl.pallas_call(functools.partial(body, (ND, NZ, NY, docs)), out_shape=jax...  60.2 us

profile of v4, /device:TPU:0, one launch (start us, length us, event | category | flops | bytes accessed | tf_op | source)
XLA Modules:
  0.0 62.1 jit_solution(13959550566891568391)
XLA Ops:
  0.6 60.2 %packed_loglik.1.packed = f32[8,128]{1,0:T(8,128)} custom-call(bf16[56,2048]{1,0:T(8,128)(2,1)} %q_hbm.1, bf16[56,1024]{1,0:T(8,128)(2,1)} %k_hbm.1, bf16[56,1024]{1,0:T(8,128)(2,1)} %v_hbm.1, bf16[4096,1792]{1,0:T(8,128)(2,1)} %w_hbm.1, bf16[56,1792]{1,0:T(8,128)(2,1)} %res_hbm.1, f32[1792]{0:T(1024)} %pg_hbm.1, f32[1792]{0:T(1024)} %fg_hbm.1, ...), custom_call_target="tpu_custom_call" | custom-call | tf_op jit(solution)/shard_map/packed_loglik/pallas_call | solution.py:777
  60.9 1.2 %split.1 = (f32[1,56]{1,0:T(1,128)}, f32[1,32]{1,0:T(1,128)}, f32[1,32]{1,0:T(1,128)}) custom-call(f32[8,128]{1,0:T(8,128)} %packed_loglik.1.packed), custom_call_target="tpu_custom_call" | custom-call | tf_op jit(solution)/shard_map/split/pallas_call | solution.py:834

commit v5 on v4

--- a/solution.py
+++ b/solution.py
@@ -562,18 +562,23 @@
         def _(n=n):
             spread(n, start, True)
 
+    for n in range(2, NZ):
+        @pl.when((n == me_z + 1) & jnp.logical_not(bottom | helper))
+        def _(n=n):
+            spread(n, start, True)
+
     if NZ > 1:
         @pl.when(under)
         def _():
             relay(1, start, True)
 
-    if NZ > 3:
-        @pl.when(me_z == NZ - 2)
+    if NZ > 2:
+        @pl.when(helper)
         def _():
             spread(NZ - 1, start, True)
 
     for n in range(2, NZ):
-        @pl.when((n > me_z) & ((n < NZ - 1) | (me_z != NZ - 2) | (NZ == 3)))
+        @pl.when((n > me_z + 1) | ((n > me_z) & bottom & jnp.logical_not(helper)))
         def _(n=n):
             spread(n, start, True)
 
@@ -588,8 +593,10 @@
         @pl.when(under)
         def _(n=n):
             if n == 2:
-                lift(start)
+                pl.when(helper)(lambda: lift(start))
             relay(n, start, True)
+            if n == 2:
+                pl.when(jnp.logical_not(helper))(lambda: lift(start))
 
     if NZ < 3:
         begin_slice(0)

time: 62.3 us -> 61.3 us (0.984)
  Pallas kernels: 61.4 us -> 60.4 us
    pallas_call x1, Pallas kernels: 60.2 us -> 59.3 us  [local(): pl.pallas_call(functools.partial(body, (ND, NZ, NY, docs)), out_shape=jax...]
where the time goes in v5:
time: 61.3 us; the launch traced here: 61.1 us
  Pallas kernels  60.4 us (99%)
  between operations  0.64 us (1%)
    pallas_call x1, Pallas kernels, local(): pl.pallas_call(functools.partial(body, (ND, NZ, NY, docs)), out_shape=jax...  59.3 us

profile of v5, /device:TPU:0, one launch (start us, length us, event | category | flops | bytes accessed | tf_op | source)
XLA Modules:
  0.0 61.1 jit_solution(11718085777897916213)
XLA Ops:
  0.6 59.3 %packed_loglik.1.packed = f32[8,128]{1,0:T(8,128)} custom-call(bf16[56,2048]{1,0:T(8,128)(2,1)} %q_hbm.1, bf16[56,1024]{1,0:T(8,128)(2,1)} %k_hbm.1, bf16[56,1024]{1,0:T(8,128)(2,1)} %v_hbm.1, bf16[4096,1792]{1,0:T(8,128)(2,1)} %w_hbm.1, bf16[56,1792]{1,0:T(8,128)(2,1)} %res_hbm.1, f32[1792]{0:T(1024)} %pg_hbm.1, f32[1792]{0:T(1024)} %fg_hbm.1, ...), custom_call_target="tpu_custom_call" | custom-call | tf_op jit(solution)/shard_map/packed_loglik/pallas_call | solution.py:784
  59.9 1.2 %split.1 = (f32[1,56]{1,0:T(1,128)}, f32[1,32]{1,0:T(1,128)}, f32[1,32]{1,0:T(1,128)}) custom-call(f32[8,128]{1,0:T(8,128)} %packed_loglik.1.packed), custom_call_target="tpu_custom_call" | custom-call | tf_op jit(solution)/shard_map/split/pallas_call | solution.py:841

commit v6 on v5

--- a/solution.py
+++ b/solution.py
@@ -546,14 +546,14 @@
 
     spread(0, start, True)
 
-    @pl.when(bottom)
+    @pl.when(bottom | helper)
     def _():
         relay(0, start, True)
 
     if NZ > 1:
         spread(1, start, True)
 
-        @pl.when(jnp.logical_not(bottom))
+        @pl.when(jnp.logical_not(bottom | helper))
         def _():
             relay(0, start, True)
 

time: 61.3 us -> 64.9 us (1.059)
  Pallas kernels: 60.4 us -> 64 us
    pallas_call x1, Pallas kernels: 59.3 us -> 62.8 us  [local(): pl.pallas_call(functools.partial(body, (ND, NZ, NY, docs)), out_shape=jax...]
where the time goes in v6:
time: 64.9 us; the launch traced here: 64.7 us
  Pallas kernels  64 us (99%)
    pallas_call x1, Pallas kernels, local(): pl.pallas_call(functools.partial(body, (ND, NZ, NY, docs)), out_shape=jax...  62.8 us

profile of v6, /device:TPU:0, one launch (start us, length us, event | category | flops | bytes accessed | tf_op | source)
XLA Modules:
  0.0 64.7 jit_solution(13480450974666807560)
XLA Ops:
  0.6 62.8 %packed_loglik.1.packed = f32[8,128]{1,0:T(8,128)} custom-call(bf16[56,2048]{1,0:T(8,128)(2,1)} %q_hbm.1, bf16[56,1024]{1,0:T(8,128)(2,1)} %k_hbm.1, bf16[56,1024]{1,0:T(8,128)(2,1)} %v_hbm.1, bf16[4096,1792]{1,0:T(8,128)(2,1)} %w_hbm.1, bf16[56,1792]{1,0:T(8,128)(2,1)} %res_hbm.1, f32[1792]{0:T(1024)} %pg_hbm.1, f32[1792]{0:T(1024)} %fg_hbm.1, ...), custom_call_target="tpu_custom_call" | custom-call | tf_op jit(solution)/shard_map/packed_loglik/pallas_call | solution.py:784
  63.5 1.2 %split.1 = (f32[1,56]{1,0:T(1,128)}, f32[1,32]{1,0:T(1,128)}, f32[1,32]{1,0:T(1,128)}) custom-call(f32[8,128]{1,0:T(8,128)} %packed_loglik.1.packed), custom_call_target="tpu_custom_call" | custom-call | tf_op jit(solution)/shard_map/split/pallas_call | solution.py:841
